TPU v7x, 128 devices: a whole 4x4x4 slice. The times are simulated.
128 devices in a mesh: batch: 1, head: 2 (over core), seq: 64 (over z, y, x).
Axes of the slice: x: 4, y: 4, z: 4, core: 2. Of those that a mesh axis runs over, the one named last changes fastest.
Arguments:
- x_embed: bfloat16 [16384, 2048], P(('batch', 'seq'))
- positions: int32 [16384], P(('batch', 'seq'))
- w_q: bfloat16 [2, 2048, 32, 64], P(None, None, 'head')
- w_k: bfloat16 [2, 2048, 8, 64], P(None, None, 'head')
- w_v: bfloat16 [2, 2048, 8, 64], P(None, None, 'head')
- w_o: bfloat16 [2, 32, 64, 2048], P(None, 'head')
- w_gate: bfloat16 [2, 2048, 8192], P(None, None, 'head')
- w_up: bfloat16 [2, 2048, 8192], P(None, None, 'head')
- w_down: bfloat16 [2, 8192, 2048], P(None, 'head')
- norm_gain: bfloat16 [2, 2048], replicated
Outputs:
- output 1: bfloat16 [16384, 2048], P(('batch', 'seq'))
- output 2: bfloat16 [2, 16384, 8, 64], P(None, ('batch', 'seq'), 'head')
- output 3: bfloat16 [2, 16384, 8, 64], P(None, ('batch', 'seq'), 'head')
All inputs are finite; a program needn't handle non-finite values.
Results may differ from a plain program's by a relative error of at most 0.02.
Values are sent between devices in bfloat16 or wider.
A program may use at most 1 GiB of HBM per device.

v0:
```python
import math
import jax
import jax.numpy as jnp
from jax import lax
from jax.sharding import PartitionSpec as P

ROPE_BASE = 500000.0
EPS = 1e-5


def rms_norm(x_in, gain_row):
    x_f32 = x_in.astype(jnp.float32)
    inv_rms = lax.rsqrt(jnp.mean(x_f32 * x_f32, axis=-1, keepdims=True) + EPS)
    return (x_f32 * inv_rms * gain_row.astype(jnp.float32)).astype(jnp.bfloat16)


def rope_tables(positions, head_dim):
    half_dim = head_dim // 2
    inv_freq = ROPE_BASE ** (-(jnp.arange(half_dim, dtype=jnp.float32) * 2.0 / head_dim))
    angles = positions.astype(jnp.float32)[..., None] * inv_freq
    return jnp.cos(angles), jnp.sin(angles)


def apply_rope(heads_in, cos_t, sin_t):
    half_dim = heads_in.shape[-1] // 2
    heads_f32 = heads_in.astype(jnp.float32)
    first_half = heads_f32[..., :half_dim]
    second_half = heads_f32[..., half_dim:]
    cos_b = cos_t[..., None, :]
    sin_b = sin_t[..., None, :]
    rotated = jnp.concatenate([first_half * cos_b - second_half * sin_b, second_half * cos_b + first_half * sin_b], axis=-1)
    return rotated.astype(jnp.bfloat16)


def block_update(soft_state, q_rot, k_blk, v_blk, row_index, col_index, logit_scale):
    row_max, row_sum, accum_out = soft_state
    logits = jnp.einsum('qkgd,skd->qkgs', q_rot, k_blk, preferred_element_type=jnp.float32) * logit_scale
    allowed = (row_index[:, None] >= col_index[None, :])[:, None, None, :]
    logits = jnp.where(allowed, logits, -jnp.inf)
    new_max = jnp.maximum(row_max, jnp.max(logits, axis=-1))
    prob_f32 = jnp.exp(logits - new_max[..., None])
    rescale = jnp.exp(row_max - new_max)
    row_sum = row_sum * rescale + jnp.sum(prob_f32, axis=-1)
    pv_part = jnp.einsum('qkgs,skd->qkgd', prob_f32.astype(jnp.bfloat16), v_blk, preferred_element_type=jnp.float32)
    accum_out = accum_out * rescale[..., None] + pv_part
    return new_max, row_sum, accum_out


def passed_attention(q_rot, k_rot, v_heads, seq_count):
    tok_count, kv_local, group_size, head_dim = q_rot.shape
    my_index = lax.axis_index('seq')
    logit_scale = 1.0 / math.sqrt(head_dim)
    local_index = jnp.arange(tok_count)
    row_index = my_index * tok_count + local_index
    shift_pairs = [(sender, (sender + 1) % seq_count) for sender in range(seq_count)]
    stat_shape = (tok_count, kv_local, group_size)
    init_state = (jnp.full(stat_shape, -jnp.inf, jnp.float32), jnp.zeros(stat_shape, jnp.float32), jnp.zeros(stat_shape + (head_dim,), jnp.float32))
    first_state = block_update(init_state, q_rot, k_rot, v_heads, row_index, row_index, logit_scale)

    def pass_step(step_num, loop_carry):
        k_blk, v_blk, state_in = loop_carry
        k_blk = lax.ppermute(k_blk, 'seq', shift_pairs)
        v_blk = lax.ppermute(v_blk, 'seq', shift_pairs)
        src_index = (my_index - step_num) % seq_count
        col_index = src_index * tok_count + local_index
        return k_blk, v_blk, block_update(state_in, q_rot, k_blk, v_blk, row_index, col_index, logit_scale)

    final_carry = lax.fori_loop(1, seq_count, pass_step, (k_rot, v_heads, first_state))
    row_max, row_sum, accum_out = final_carry[2]
    attn_heads = (accum_out / row_sum[..., None]).astype(jnp.bfloat16)
    return attn_heads.reshape(tok_count, kv_local * group_size * head_dim)


def solution(mesh):
    seq_count = mesh.shape['seq']
    row_spec = P(('batch', 'seq'), None)
    pos_spec = P(('batch', 'seq'))
    head_spec = P(None, None, 'head', None)
    out_proj_spec = P(None, 'head', None, None)
    col_spec = P(None, None, 'head')
    down_spec = P(None, 'head', None)
    cache_spec = P(None, ('batch', 'seq'), 'head', None)

    def local_forward(x_loc, pos_loc, w_q, w_k, w_v, w_o, w_gate, w_up, w_down, norm_gain):
        tok_count, d_model = x_loc.shape
        layer_count = w_q.shape[0]
        q_local = w_q.shape[2]
        head_dim = w_q.shape[3]
        kv_local = w_k.shape[2]
        group_size = q_local // kv_local
        cos_t, sin_t = rope_tables(pos_loc, head_dim)
        x_cur = x_loc
        k_list = []
        v_list = []
        for layer in range(layer_count):
            normed = rms_norm(x_cur, norm_gain[layer])
            q_proj = jnp.dot(normed, w_q[layer].reshape(d_model, q_local * head_dim), preferred_element_type=jnp.float32).astype(jnp.bfloat16)
            k_proj = jnp.dot(normed, w_k[layer].reshape(d_model, kv_local * head_dim), preferred_element_type=jnp.float32).astype(jnp.bfloat16)
            v_proj = jnp.dot(normed, w_v[layer].reshape(d_model, kv_local * head_dim), preferred_element_type=jnp.float32).astype(jnp.bfloat16)
            q_rot = apply_rope(q_proj.reshape(tok_count, q_local, head_dim), cos_t, sin_t).reshape(tok_count, kv_local, group_size, head_dim)
            k_rot = apply_rope(k_proj.reshape(tok_count, kv_local, head_dim), cos_t, sin_t)
            v_heads = v_proj.reshape(tok_count, kv_local, head_dim)
            attn_heads = passed_attention(q_rot, k_rot, v_heads, seq_count)
            part_sum = jnp.dot(attn_heads, w_o[layer].reshape(q_local * head_dim, d_model), preferred_element_type=jnp.float32)
            gate_f32 = jnp.dot(normed, w_gate[layer], preferred_element_type=jnp.float32)
            up_f32 = jnp.dot(normed, w_up[layer], preferred_element_type=jnp.float32)
            hidden = (jax.nn.silu(gate_f32) * up_f32).astype(jnp.bfloat16)
            part_sum = part_sum + jnp.dot(hidden, w_down[layer], preferred_element_type=jnp.float32)
            update = lax.psum(part_sum, 'head').astype(jnp.bfloat16)
            x_cur = (x_cur.astype(jnp.float32) + update.astype(jnp.float32)).astype(jnp.bfloat16)
            k_list.append(k_rot)
            v_list.append(v_heads)
        return x_cur, jnp.stack(k_list), jnp.stack(v_list)

    return jax.shard_map(local_forward, mesh=mesh, in_specs=(row_spec, pos_spec, head_spec, head_spec, head_spec, out_proj_spec, col_spec, col_spec, down_spec, P(None, None)), out_specs=(row_spec, cache_spec, cache_spec), check_vma=False)
```

profile of v0, /device:TPU:121, one launch (start us, length us, event | category | flops | bytes accessed | tf_op | source)
XLA Modules:
  0.0 1884.6 jit_solution(1184466905691964938)
XLA Ops:
  19.8 860.6 %while.48 = (s32[]{:T(128)}, bf16[256,4,64]{0,2,1:T(8,128)(2,1)}, bf16[256,4,64]{0,2,1:T(8,128)(2,1)S(1)}, f32[256,4,4]{0,2,1:T(4,128)S(1)}, f32[256,4,4]{0,2,1:...) while((s32[]{:T(128)}, bf16[256,4,64]{0,2,1:T(8,128)(2,1)}, ...), condition=%wide.region_6.7_spmd.clone, body=%wide.region_3.6_spmd.clone.sunk | while | flops 280568320 | bytes 17568096 | solution.py:68
  194.3 7.4 collective-permute-start.1
  236.5 7.4 collective-permute-start.1
  250.6 7.4 collective-permute-start.1
  264.6 7.4 collective-permute-start.1
  278.7 7.4 collective-permute-start.1
  292.8 7.4 collective-permute-start.1
  306.8 7.4 collective-permute-start.1
  320.9 7.4 collective-permute-start.1
  377.1 7.4 collective-permute-start.1
  391.2 7.4 collective-permute-start.1
  405.3 7.4 collective-permute-start.1
  419.3 7.4 collective-permute-start.1
  433.4 7.4 collective-permute-start.1
  447.5 7.4 collective-permute-start.1
  461.5 7.4 collective-permute-start.1
  503.7 7.4 collective-permute-start.1
  517.8 7.4 collective-permute-start.1
  531.8 7.4 collective-permute-start.1
  545.9 7.4 collective-permute-start.1
  560.0 7.4 collective-permute-start.1
  574.0 7.4 collective-permute-start.1
  588.1 7.4 collective-permute-start.1
  644.3 7.4 collective-permute-start.1
  658.4 7.4 collective-permute-start.1
  672.5 7.4 collective-permute-start.1
  888.5 12.3 fusion.52
  900.8 18.1 fusion.78
  919.0 22.1 %all-reduce.2 = bf16[256,2048]{1,0:T(8,128)(2,1)S(1)} all-reduce(f32[256,2048]{1,0:T(8,128)} %fusion.78), channel_id=1, replica_groups=mesh['batch'=1,'head'=2,'seq'=64] {'head'}, use_global_device_ids=true, to_apply=%region_7.8 | all-reduce | flops 524288 | bytes 3145728 | tf_op jit(solution)/shard_map/psum | solution.py:109
  945.0 12.5 fusion.46
  962.1 829.5 %while.49 = (s32[]{:T(128)}, bf16[256,4,64]{0,2,1:T(8,128)(2,1)S(1)}, bf16[256,4,64]{0,2,1:T(8,128)(2,1)S(1)}, f32[256,4,4]{0,2,1:T(4,128)S(1)}, f32[256,4,4]{0,...) while((s32[]{:T(128)}, ...), condition=%wide.region_14.15_spmd.clone, body=%wide.region_11.14_spmd.clone.sunk | while | flops 280568320 | bytes 17568096 | solution.py:68
  964.6 7.5 collective-permute-start.3
  991.9 7.6 collective-permute-start.3
  1119.7 7.4 collective-permute-start.3
  1134.5 7.4 collective-permute-start.3
  1162.2 7.4 collective-permute-start.3
  1174.9 7.7 collective-permute-start.3
  1317.0 7.4 collective-permute-start.3
  1331.8 7.5 collective-permute-start.3
  1359.5 7.6 collective-permute-start.3
  1487.4 7.4 collective-permute-start.3
  1529.9 7.4 collective-permute-start.3
  1542.5 7.7 collective-permute-start.3
  1712.7 7.4 collective-permute-start.3
  1740.8 7.7 collective-permute-start.3
  1779.5 7.9 collective-permute-start.3
  1796.6 18.1 fusion.81
  1814.7 68.5 %all-reduce.3 = bf16[256,2048]{1,0:T(8,128)(2,1)S(1)} all-reduce(f32[256,2048]{1,0:T(8,128)} %fusion.81), channel_id=1, replica_groups=mesh['batch'=1,'head'=2,'seq'=64] {'head'}, use_global_device_ids=true, to_apply=%region_15.16 | all-reduce | flops 524288 | bytes 3145728 | tf_op jit(solution)/shard_map/psum | solution.py:109
  (1807 shorter events, 1425.6 us)
Async XLA Ops:
  191.3 10.5 collective-permute-start
  205.4 10.5 collective-permute-start
  219.5 10.5 collective-permute-start
  233.5 10.5 collective-permute-start
  247.6 10.5 collective-permute-start
  261.7 10.5 collective-permute-start
  275.7 10.5 collective-permute-start
  289.8 10.5 collective-permute-start
  303.8 10.5 collective-permute-start
  317.9 10.5 collective-permute-start
  332.0 10.5 collective-permute-start
  346.0 10.5 collective-permute-start
  360.1 10.5 collective-permute-start
  374.2 10.5 collective-permute-start
  388.2 10.5 collective-permute-start
  402.3 10.5 collective-permute-start
  416.4 10.5 collective-permute-start
  430.4 10.5 collective-permute-start
  444.5 10.5 collective-permute-start
  458.5 10.5 collective-permute-start
  472.6 10.5 collective-permute-start
  486.7 10.5 collective-permute-start
  500.7 10.5 collective-permute-start
  514.8 10.5 collective-permute-start
  528.9 10.5 collective-permute-start
  542.9 10.5 collective-permute-start
  557.0 10.5 collective-permute-start
  571.0 10.5 collective-permute-start
  585.1 10.5 collective-permute-start
  669.5 10.5 collective-permute-start
  810.1 10.5 collective-permute-start
  988.7 10.9 collective-permute-start.2
  1105.3 10.5 collective-permute-start.3
  1131.1 11.0 collective-permute-start.2
  1145.1 10.7 collective-permute-start.2
  1158.8 10.9 collective-permute-start.2
  1328.5 11.0 collective-permute-start.2
  1342.7 10.6 collective-permute-start.2
  1356.4 10.9 collective-permute-start.2
  1473.0 10.5 collective-permute-start.3
  1498.7 11.0 collective-permute-start.2
  1512.7 10.7 collective-permute-start.2
  1526.5 10.9 collective-permute-start.2
  1709.5 10.6 collective-permute-start.2
  1723.6 10.9 collective-permute-start.2
  1737.6 10.9 collective-permute-start.2
  1751.6 10.6 collective-permute-start.2
  1779.5 11.0 collective-permute-start.3
  (222 other events, 2015.9 us)
where the time goes:
time: 1900 us; the launch traced here: 1880 us
  starting transfers between devices  1220 us (64%)
  matrix products  328 us (17%)
  other arithmetic  136 us (7%)
  blocking collectives  90.6 us (5%)
  local copies, waits for them, and re-layouts  56.6 us (3%)
  waiting for transfers between devices  45.9 us (2%)
    ppermute x126, starting transfers between devices, pass_step(): v_blk = lax.ppermute(v_blk, 'seq', shift_pairs)  879 us
    ppermute x126, starting transfers between devices, pass_step(): k_blk = lax.ppermute(k_blk, 'seq', shift_pairs)  337 us
    dot_general x128, matrix products, block_update(): jnp.einsum('qkgs,skd->qkgd', prob_f32.astype(jnp.bfloat16), v_blk, prefer...  152 us
    reduce_sum x128, other arithmetic, block_update(): row_sum = row_sum * rescale + jnp.sum(prob_f32, axis=-1)  113 us
    dot_general x128, matrix products, block_update(): jnp.einsum('qkgd,skd->qkgs', q_rot, k_blk, preferred_element_type=jnp.flo...  100 us
    psum x2, blocking collectives, local_forward(): update = lax.psum(part_sum, 'head').astype(jnp.bfloat16)  90.6 us
    while x378, local copies, waits for them, and re-layouts  43.7 us
  transfers between devices with their start and end apart: 252, of which 70 were waited for; matrix products, arithmetic and copies ran while one was open for 14% of the time, Pallas kernels for 0%

commit v1 on v0

v1 whole, which is shorter than its diff:
```python
import functools
import jax
import jax.numpy as jnp
from jax import lax
from jax.experimental import pallas as pl
from jax.experimental.pallas import tpu as pltpu
from jax.sharding import PartitionSpec as P

ROPE_BASE = 500000.0
EPS = 1e-5
LOG2E = 1.4426950408889634
NEG = -1e30
MESH = pl.DeviceIdType.MESH
F32 = jnp.float32
BF16 = jnp.bfloat16
VMEM_LIMIT = 62 * 1024 * 1024

DIM_ORDER = (((0, 1, 2), (0, 1, 2), (1, 2, 0), (2, 0, 1)), ((0, 1, 2), (1, 2, 0), (1, 2, 0), (2, 0, 1)))


def rope_tables(positions, head_dim):
    half_dim = head_dim // 2
    inv_freq = ROPE_BASE ** (-(jnp.arange(half_dim, dtype=F32) * 2.0 / head_dim))
    angles = positions.astype(F32)[..., None] * inv_freq
    return jnp.cos(angles), jnp.sin(angles)


class Place:
    def __init__(self):
        self.seq = lax.axis_index('seq')
        self.head = lax.axis_index('head')
        self.xyz = (self.seq % 4, (self.seq // 4) % 4, self.seq // 16)
        self.mem = tuple(c // 2 for c in self.xyz)
        self.cls = tuple(((c + 1) // 2) % 2 for c in self.xyz)
        self.core = (self.mem[0] + self.mem[1]) % 2
        self.kv_local = 2 * self.mem[1] + self.mem[0]
        self.member = 2 * self.mem[2] + self.mem[0]

    def is_self(self):
        same_z = 1 - lax.rem(self.head + self.mem[2], 2)
        same_c = 1 - lax.rem(self.head + self.core, 2)
        return same_z * same_c

    def at(self, mem, cls):
        cs = [m * 3 + c * (1 - 2 * m) for m, c in zip(mem, cls)]
        return cs[2] * 16 + cs[1] * 4 + cs[0]

    def target(self, t):
        return self.at((t % 2, t // 2, self.head), self.cls)

    def source_mem(self, i):
        mx, mz = i % 2, i // 2
        return (mx, (mx + self.head) % 2, mz)

    def source(self, i, flips=()):
        cls = [1 - c if d in flips else c for d, c in enumerate(self.cls)]
        return self.at(self.source_mem(i), cls)

    def partner(self, dim):
        cls = [1 - c if d == dim else c for d, c in enumerate(self.cls)]
        return self.at(self.mem, cls)

    def dev(self, seq, head):
        return {'seq': seq, 'head': head}


def rope_lanes(x, cos, sin):
    lane = lax.broadcasted_iota(jnp.int32, (x.shape[0], 128), 1)
    first = (lane % 64) < 32
    out = []
    for c in range(x.shape[1] // 128):
        part = x[:, c * 128:(c + 1) * 128]
        rot = jnp.where(first, pltpu.roll(part, 96, 1), pltpu.roll(part, 32, 1))
        out.append((part * cos + rot * sin).astype(BF16))
    return jnp.concatenate(out, axis=1)


def front_kernel(layer, x_ref, gain_ref, cos_ref, sin_ref, cosT_ref, sinT_ref, wq, wk, wv, wg, wu, wd, kT_ref, vT_ref, q_all, kv_all, mlp_ref, h_ref, q_send, kv_send, wqb, wkb, wvb, wgb, wub, wdb, wsem, msem, skv, sq, sag, sdd, rkv, rq, rag, rdd):
    me = Place()
    sib = 1 - me.head
    n_tiles = 16
    flag = me.is_self()

    barrier = pltpu.get_barrier_semaphore()
    for i in range(4):
        mem = me.source_mem(i)
        src_self = flag * (1 - lax.rem(i // 2 + me.mem[2], 2)) * (1 - lax.rem(i % 2 + me.mem[0], 2))

        @pl.when(src_self == 0)
        def _():
            pl.semaphore_signal(barrier, inc=1, device_id=me.dev(me.source(i), me.mem[2]), device_id_type=MESH)
    for d in range(3):
        pl.semaphore_signal(barrier, inc=1, device_id=me.dev(me.partner(d), me.head), device_id_type=MESH)
    pl.semaphore_signal(barrier, inc=1, device_id=me.dev(me.seq, sib), device_id_type=MESH)

    cps = [pltpu.make_async_copy(wk.at[layer], wkb, wsem.at[0]), pltpu.make_async_copy(wv.at[layer], wvb, wsem.at[1])]
    for t in range(4):
        cps.append(pltpu.make_async_copy(wq.at[layer, pl.ds(t * 256, 256)], wqb.at[t], wsem.at[2 + t]))
    for c in cps:
        c.start()

    def tile_copies(n, slot):
        return (pltpu.make_async_copy(wg.at[layer, :, pl.ds(pl.multiple_of(n * 256, 256), 256)], wgb.at[slot], msem.at[slot, 0]),
                pltpu.make_async_copy(wu.at[layer, :, pl.ds(pl.multiple_of(n * 256, 256), 256)], wub.at[slot], msem.at[slot, 1]),
                pltpu.make_async_copy(wd.at[layer, pl.ds(pl.multiple_of(n * 256, 256), 256)], wdb.at[slot], msem.at[slot, 2]))

    for n in range(3):
        for c in tile_copies(n, n):
            c.start()

    xf = x_ref[...].astype(F32)
    inv = lax.rsqrt(jnp.mean(xf * xf, axis=-1, keepdims=True) + EPS)
    h_ref[...] = (xf * inv * gain_ref[layer:layer + 1, :].astype(F32)).astype(BF16)

    nt = (((1,), (1,)), ((), ()))
    cps[0].wait()
    kT = lax.dot_general(wkb[...], h_ref[...], nt, preferred_element_type=F32).astype(BF16).astype(F32)
    cosT, sinT = cosT_ref[...], sinT_ref[...]
    for t in range(4):
        a, b = kT[t * 64:t * 64 + 32], kT[t * 64 + 32:t * 64 + 64]
        ra, rb = (a * cosT - b * sinT).astype(BF16), (b * cosT + a * sinT).astype(BF16)
        kv_send[t, 0:32, :] = ra
        kv_send[t, 32:64, :] = rb
        kT_ref[t * 64:t * 64 + 32, :] = ra
        kT_ref[t * 64 + 32:t * 64 + 64, :] = rb
    cps[1].wait()
    vT = lax.dot_general(wvb[...], h_ref[...], nt, preferred_element_type=F32).astype(BF16)
    vT_ref[...] = vT
    for t in range(4):
        kv_send[t, 64:128, :] = vT[t * 64:(t + 1) * 64]

    pl.semaphore_wait(barrier, 8 - flag)

    def kv_copy(t):
        return pltpu.make_async_remote_copy(src_ref=kv_send.at[t], dst_ref=kv_all.at[me.seq], send_sem=skv.at[t], recv_sem=rkv.at[me.member], device_id=me.dev(me.target(t), me.core), device_id_type=MESH)

    def q_copy(t):
        return pltpu.make_async_remote_copy(src_ref=q_send.at[t], dst_ref=q_all.at[me.member], send_sem=sq.at[t], recv_sem=rq.at[me.member], device_id=me.dev(me.target(t), me.core), device_id_type=MESH)

    def t_self(t):
        return flag * (1 - lax.rem(t // 2 + me.mem[1], 2)) * (1 - lax.rem(t % 2 + me.mem[0], 2))

    def send_all(make, src, dst, idx):
        for t in range(4):
            @pl.when(t_self(t) == 0)
            def _():
                make(t).start()

            @pl.when(t_self(t) == 1)
            def _():
                dst[idx] = src[t]

    send_all(kv_copy, kv_send, kv_all, me.seq)

    cos, sin = cos_ref[...], sin_ref[...]
    for t in range(4):
        cps[2 + t].wait()
        q = lax.dot_general(h_ref[...], wqb[t], nt, preferred_element_type=F32).astype(BF16).astype(F32)
        q_send[t] = rope_lanes(q, cos, sin)
    send_all(q_copy, q_send, q_all, me.member)

    def ag_plan(i):
        plans = []
        for core in range(2):
            d1, d2, d3 = DIM_ORDER[core][i]
            plans.append([(d1, ()), (d2, ()), (d2, (d1,)), (d3, ()), (d3, (d1,)), (d3, (d2,)), (d3, (d1, d2))])
        return plans

    def ag_copy(core, i, k):
        dim, flips = ag_plan(i)[core][k]
        pos = me.source(i, flips)
        return pltpu.make_async_remote_copy(src_ref=kv_all.at[pos], dst_ref=kv_all.at[pos], send_sem=sag.at[i, k], recv_sem=rag.at[i, k], device_id=me.dev(me.partner(dim), me.head), device_id_type=MESH)

    def got_flips(core, i, k):
        dim, flips = ag_plan(i)[core][k]
        return tuple(flips) + (dim,)

    def ag_recv(core, i, k):
        pos = me.source(i, got_flips(core, i, k))
        pltpu.make_async_remote_copy(src_ref=kv_all.at[pos], dst_ref=kv_all.at[pos], send_sem=sag.at[i, k], recv_sem=rag.at[i, k], device_id=me.dev(me.seq, sib), device_id_type=MESH).wait_recv()

    def dd_copy(pos, i, k):
        return pltpu.make_async_remote_copy(src_ref=kv_all.at[pos], dst_ref=kv_all.at[pos], send_sem=sdd.at[i, k], recv_sem=rdd.at[i, k], device_id=me.dev(me.seq, sib), device_id_type=MESH)

    def s_self(i):
        return flag * (1 - lax.rem(i // 2 + me.mem[2], 2)) * (1 - lax.rem(i % 2 + me.mem[0], 2))

    def per_core(fn):
        for core in range(2):
            @pl.when(me.head == core)
            def _():
                fn(core)

    def phase1(core):
        for i in range(4):
            @pl.when(s_self(i) == 0)
            def _():
                pltpu.make_async_remote_copy(src_ref=kv_send.at[0], dst_ref=kv_all.at[me.source(i)], send_sem=skv.at[0], recv_sem=rkv.at[i], device_id=me.dev(me.seq, sib), device_id_type=MESH).wait_recv()
            ag_copy(core, i, 0).start()
        for k in (1, 3):
            for i in range(4):
                ag_copy(core, i, k).start()
        for i in range(4):
            dd_copy(me.source(i), i, 0).start()

    def phase2(core):
        for i in range(4):
            ag_recv(core, i, 0)
            ag_copy(core, i, 2).start()
            ag_copy(core, i, 4).start()
            dd_copy(me.source(i, got_flips(core, i, 0)), i, 1).start()
        for i in range(4):
            ag_recv(core, i, 1)
            ag_copy(core, i, 5).start()
            dd_copy(me.source(i, got_flips(core, i, 1)), i, 2).start()

    def phase3(core):
        for i in range(4):
            ag_recv(core, i, 2)
            ag_copy(core, i, 6).start()
            dd_copy(me.source(i, got_flips(core, i, 2)), i, 3).start()

    def phase4(core):
        for k in range(3, 7):
            for i in range(4):
                ag_recv(core, i, k)
                dd_copy(me.source(i, got_flips(core, i, k)), i, k + 1).start()

    def phase5(core):
        other = 1 - core
        for k in range(8):
            for i in range(4):
                mx, mz = i % 2, i // 2
                mem = (mx, (mx + other) % 2, mz)
                flips = () if k == 0 else got_flips(other, i, k - 1)
                cls = [1 - c if d in flips else c for d, c in enumerate(me.cls)]
                dd_copy(me.at(mem, cls), i, k).wait_recv()
        for i in range(4):
            for k in range(7):
                ag_copy(core, i, k).wait_send()
            for k in range(8):
                dd_copy(me.source(i), i, k).wait_send()

    mlp_ref[...] = jnp.zeros_like(mlp_ref)

    def tile(n, carry):
        slot = n % 3
        for c in tile_copies(n, slot):
            c.wait()
        for at, fn in ((4, phase1), (9, phase2), (13, phase3)):
            @pl.when(n == at)
            def _():
                per_core(fn)
        g = jnp.dot(h_ref[...], wgb[slot], preferred_element_type=F32)
        u = jnp.dot(h_ref[...], wub[slot], preferred_element_type=F32)
        hid = (g * jax.nn.sigmoid(g) * u).astype(BF16)
        mlp_ref[...] += jnp.dot(hid, wdb[slot], preferred_element_type=F32)

        @pl.when(n + 3 < n_tiles)
        def _():
            for c in tile_copies(n + 3, slot):
                c.start()
        return carry

    lax.fori_loop(0, n_tiles, tile, 0)
    per_core(phase4)
    per_core(phase5)
    for t in range(4):
        @pl.when(t_self(t) == 0)
        def _():
            kv_copy(t).wait_send()
            q_copy(t).wait_send()
    for i in range(4):
        @pl.when(s_self(i) == 0)
        def _():
            pltpu.make_async_remote_copy(src_ref=q_send.at[0], dst_ref=q_all.at[i], send_sem=sq.at[0], recv_sem=rq.at[i], device_id=me.dev(me.seq, sib), device_id_type=MESH).wait_recv()


def attn_tile(q, kT, vT, m_ref, l_ref, acc_ref, rows, mask=None):
    s = jnp.dot(q, kT, preferred_element_type=F32) * (LOG2E / 8.0)
    if mask is not None:
        s = jnp.where(mask, s, NEG)
    m_old = m_ref[rows, :]
    m_new = jnp.maximum(m_old, jnp.broadcast_to(jnp.max(s, axis=1, keepdims=True), m_old.shape))
    alpha = jnp.exp2(m_old - m_new)
    lsum = l_ref[rows, :] * alpha
    ps = []
    for c in range(s.shape[1] // 128):
        p = jnp.exp2(s[:, c * 128:(c + 1) * 128] - m_new)
        lsum = lsum + p
        ps.append(p.astype(BF16))
    l_ref[rows, :] = lsum
    pv = lax.dot_general(jnp.concatenate(ps, axis=1), vT, (((1,), (1,)), ((), ())), preferred_element_type=F32)
    acc_ref[rows, :] = acc_ref[rows, :] * alpha[:, :64] + pv
    m_ref[rows, :] = m_new


def attn_kernel(q_ref, kv_ref, o_ref, qp, m_ref, l_ref, acc_ref):
    me = Place()
    nb, mc = 4, 512

    def block(i, carry):
        pos = me.source(i)
        qb = q_ref[i]
        for g in range(4):
            qp[pl.ds(g * 256, 256), :] = qb[:, g * 64:(g + 1) * 64]
        m_ref[...] = jnp.full_like(m_ref, NEG)
        l_ref[...] = jnp.zeros_like(l_ref)
        acc_ref[...] = jnp.zeros_like(acc_ref)

        def wide(n, c):
            kT = jnp.concatenate([kv_ref[n * nb + b, :64, :] for b in range(nb)], axis=1)
            vT = jnp.concatenate([kv_ref[n * nb + b, 64:, :] for b in range(nb)], axis=1)
            for r in range(1024 // mc):
                rows = pl.ds(r * mc, mc)
                attn_tile(qp[rows, :], kT, vT, m_ref, l_ref, acc_ref, rows)
            return c

        lax.fori_loop(0, pos // nb, wide, 0)

        def narrow(n, c):
            for r in range(1024 // mc):
                rows = pl.ds(r * mc, mc)
                attn_tile(qp[rows, :], kv_ref[n, :64, :], kv_ref[n, 64:, :], m_ref, l_ref, acc_ref, rows)
            return c

        lax.fori_loop((pos // nb) * nb, pos, narrow, 0)
        ri = lax.broadcasted_iota(jnp.int32, (256, 256), 0)
        ci = lax.broadcasted_iota(jnp.int32, (256, 256), 1)
        for g in range(4):
            rows = pl.ds(g * 256, 256)
            attn_tile(qp[rows, :], kv_ref[pos, :64, :], kv_ref[pos, 64:, :], m_ref, l_ref, acc_ref, rows, ri >= ci)
        outs = []
        for g in range(4):
            rows = pl.ds(g * 256, 256)
            l = jnp.sum(l_ref[rows, :], axis=1, keepdims=True)
            outs.append((acc_ref[rows, :] / l).astype(BF16))
        o_ref[i] = jnp.concatenate(outs, axis=1)
        return carry

    lax.fori_loop(0, 4, block, 0)


def back_kernel(layer, o_ref, mlp_ref, x_ref, wo, out_ref, o_full, part, part_in, wob, wsem, so, ro, sp, rp):
    me = Place()
    sib = 1 - me.head
    flag = me.is_self()
    barrier = pltpu.get_barrier_semaphore()

    def s_self(i):
        return flag * (1 - lax.rem(i // 2 + me.mem[2], 2)) * (1 - lax.rem(i % 2 + me.mem[0], 2))

    def t_self(t):
        return flag * (1 - lax.rem(t // 2 + me.mem[1], 2)) * (1 - lax.rem(t % 2 + me.mem[0], 2))

    for t in range(4):
        @pl.when(t_self(t) == 0)
        def _():
            pl.semaphore_signal(barrier, inc=1, device_id=me.dev(me.target(t), me.core), device_id_type=MESH)
    pl.semaphore_signal(barrier, inc=1, device_id=me.dev(me.seq, sib), device_id_type=MESH)
    wcps = [pltpu.make_async_copy(wo.at[layer, pl.ds(t * 256, 256)], wob.at[t], wsem.at[t]) for t in range(4)]
    for c in wcps:
        c.start()
    pl.semaphore_wait(barrier, 5 - flag)

    def o_copy(i):
        return pltpu.make_async_remote_copy(src_ref=o_ref.at[i], dst_ref=o_full.at[me.kv_local], send_sem=so.at[i], recv_sem=ro.at[me.kv_local], device_id=me.dev(me.source(i), me.mem[2]), device_id_type=MESH)

    for i in range(4):
        @pl.when(s_self(i) == 0)
        def _():
            o_copy(i).start()

        @pl.when(s_self(i) == 1)
        def _():
            o_full[me.kv_local] = o_ref[i]
    for t in range(4):
        wcps[t].wait()
    for t in range(4):
        @pl.when(t_self(t) == 0)
        def _():
            pltpu.make_async_remote_copy(src_ref=o_ref.at[0], dst_ref=o_full.at[t], send_sem=so.at[0], recv_sem=ro.at[t], device_id=me.dev(me.seq, sib), device_id_type=MESH).wait_recv()

    def p_copy(n):
        return pltpu.make_async_remote_copy(src_ref=part.at[n], dst_ref=part_in.at[n], send_sem=sp.at[n], recv_sem=rp.at[n], device_id=me.dev(me.seq, sib), device_id_type=MESH)

    for n in range(8):
        cols = pl.ds(n * 256, 256)
        acc = mlp_ref[:, cols]
        for t in range(4):
            acc = acc + jnp.dot(o_full[t], wob[t, :, cols], preferred_element_type=F32)
        part[n] = acc
        p_copy(n).start()
    for n in range(8):
        cols = pl.ds(n * 256, 256)
        p_copy(n).wait_recv()
        y = (part[n] + part_in[n]).astype(BF16)
        out_ref[:, cols] = (x_ref[:, cols].astype(F32) + y.astype(F32)).astype(BF16)
    for n in range(8):
        p_copy(n).wait_send()
    for i in range(4):
        @pl.when(s_self(i) == 0)
        def _():
            o_copy(i).wait_send()


def vm():
    return pl.BlockSpec(memory_space=pltpu.VMEM)


def hbm():
    return pl.BlockSpec(memory_space=pl.ANY)


def sds(shape, dtype):
    return jax.ShapeDtypeStruct(shape, dtype)


def dma(*shape):
    return pltpu.SemaphoreType.DMA(shape)


def solution(mesh):
    row_spec = P(('batch', 'seq'), None)
    pos_spec = P(('batch', 'seq'))
    head_spec = P(None, None, 'head', None)
    out_proj_spec = P(None, 'head', None, None)
    col_spec = P(None, None, 'head')
    down_spec = P(None, 'head', None)
    cache_spec = P(None, ('batch', 'seq'), 'head', None)

    def local_forward(x, pos, w_q, w_k, w_v, w_o, w_gate, w_up, w_down, gain):
        cos, sin = rope_tables(pos, 64)
        cos_l = jnp.concatenate([cos] * 4, axis=1)
        sin_l = jnp.concatenate([-sin, sin, -sin, sin], axis=1)
        cosT, sinT = cos.T, sin.T
        wq = w_q.transpose(0, 2, 3, 1).reshape(2, 1024, 2048)
        wk = w_k.transpose(0, 2, 3, 1).reshape(2, 256, 2048)
        wv = w_v.transpose(0, 2, 3, 1).reshape(2, 256, 2048)
        wo = w_o.reshape(2, 1024, 2048)
        ks, vs = [], []
        for layer in range(2):
            kT, vT, q_all, kv_all, mlp = pl.pallas_call(
                functools.partial(front_kernel, layer),
                out_shape=(sds((256, 256), BF16), sds((256, 256), BF16), sds((4, 256, 256), BF16), sds((64, 128, 256), BF16), sds((256, 2048), F32)),
                in_specs=[vm()] * 6 + [hbm()] * 6,
                out_specs=[vm()] * 5,
                scratch_shapes=[
                    pltpu.VMEM((256, 2048), BF16), pltpu.VMEM((4, 256, 256), BF16), pltpu.VMEM((4, 128, 256), BF16),
                    pltpu.VMEM((4, 256, 2048), BF16), pltpu.VMEM((256, 2048), BF16), pltpu.VMEM((256, 2048), BF16),
                    pltpu.VMEM((3, 2048, 256), BF16), pltpu.VMEM((3, 2048, 256), BF16), pltpu.VMEM((3, 256, 2048), BF16),
                    dma(6), dma(3, 3), dma(4), dma(4), dma(4, 7), dma(4, 8), dma(4), dma(4), dma(4, 7), dma(4, 8)],
                compiler_params=pltpu.CompilerParams(collective_id=2 * layer, has_side_effects=True, vmem_limit_bytes=VMEM_LIMIT),
                name=f'front{layer}',
            )(x, gain, cos_l, sin_l, cosT, sinT, wq, wk, wv, w_gate, w_up, w_down)
            o = pl.pallas_call(
                attn_kernel,
                out_shape=sds((4, 256, 256), BF16),
                in_specs=[vm()] * 2,
                out_specs=vm(),
                scratch_shapes=[pltpu.VMEM((1024, 64), BF16), pltpu.VMEM((1024, 128), F32), pltpu.VMEM((1024, 128), F32), pltpu.VMEM((1024, 64), F32)],
                compiler_params=pltpu.CompilerParams(vmem_limit_bytes=VMEM_LIMIT),
                name='attn',
            )(q_all, kv_all)
            x = pl.pallas_call(
                functools.partial(back_kernel, layer),
                out_shape=sds((256, 2048), BF16),
                in_specs=[vm()] * 3 + [hbm()],
                out_specs=vm(),
                scratch_shapes=[pltpu.VMEM((4, 256, 256), BF16), pltpu.VMEM((8, 256, 256), F32), pltpu.VMEM((8, 256, 256), F32), pltpu.VMEM((4, 256, 2048), BF16),
                                dma(4), dma(4), dma(4), dma(8), dma(8)],
                compiler_params=pltpu.CompilerParams(collective_id=2 * layer + 1, has_side_effects=True, vmem_limit_bytes=VMEM_LIMIT),
                name=f'back{layer}',
            )(o, mlp, x, wo)
            ks.append(kT)
            vs.append(vT)
        k_cache = jnp.stack(ks).reshape(2, 4, 64, 256).transpose(0, 3, 1, 2)
        v_cache = jnp.stack(vs).reshape(2, 4, 64, 256).transpose(0, 3, 1, 2)
        return x, k_cache, v_cache

    return jax.shard_map(local_forward, mesh=mesh, in_specs=(row_spec, pos_spec, head_spec, head_spec, head_spec, out_proj_spec, col_spec, col_spec, down_spec, P(None, None)), out_specs=(row_spec, cache_spec, cache_spec), check_vma=False)
```

time: 1900 us -> 246 us (0.13)
  starting transfers between devices: 1220 us -> 0 us
  matrix products: 328 us -> 0 us
  Pallas kernels: 0 us -> 234 us
  other arithmetic: 136 us -> 4.48 us
  blocking collectives: 90.6 us -> 0 us
  local copies, waits for them, and re-layouts: 56.6 us -> 2.32 us
  waiting for transfers between devices: 45.9 us -> 0 us
    ppermute x252 -> x0, starting transfers between devices: 1220 us -> none  [the longest x126 879 us: pass_step(): v_blk = lax.ppermute(v_blk, 'seq', shift_pairs)]
    dot_general x268 -> x0, matrix products: 328 us -> none  [the longest x128 152 us: block_update(): jnp.einsum('qkgs,skd->qkgd', prob_f32.astype(jnp.bfloat16), v_blk, prefer...]
    pallas_call x0 -> x6, Pallas kernels: none -> 234 us  [the longest x2 122 us: local_forward(): pl.pallas_call(attn_kernel, out_shape=sds((4, 256, 256), BF16), in_specs=...]
    reduce_sum x130 -> x0, other arithmetic: 115 us -> none  [the longest x128 113 us: block_update(): row_sum = row_sum * rescale + jnp.sum(prob_f32, axis=-1)]
    psum x2 -> x0, blocking collectives: 90.6 us -> none  [local_forward(): update = lax.psum(part_sum, 'head').astype(jnp.bfloat16)]
    ppermute x252 -> x0, waiting for transfers between devices: 45.9 us -> none  [the longest x126 30.2 us: pass_step(): v_blk = lax.ppermute(v_blk, 'seq', shift_pairs)]
    while x378 -> x0, local copies, waits for them, and re-layouts: 43.7 us -> none
  transfers between devices with their start and end apart: 252 -> 0, of which waited for: 70 -> 0; matrix products, arithmetic and copies ran while one was open for 14% -> 0% of each run, Pallas kernels for 0% -> 0%
where the time goes in v1:
time: 246 us; the launch traced here: 242 us
  Pallas kernels  234 us (95%)
  other arithmetic  4.48 us (2%)
    pallas_call x2, Pallas kernels, local_forward(): pl.pallas_call(attn_kernel, out_shape=sds((4, 256, 256), BF16), in_specs=...  122 us
    pallas_call x2, Pallas kernels, local_forward(): pl.pallas_call(functools.partial(front_kernel, layer), out_shape=(sds((25...  70 us
    pallas_call x2, Pallas kernels, local_forward(): pl.pallas_call(functools.partial(back_kernel, layer), out_shape=sds((256,...  42.6 us

profile of v1, /device:TPU:121, one launch (start us, length us, event | category | flops | bytes accessed | tf_op | source)
XLA Modules:
  0.0 241.9 jit_solution(9066108825834334466)
XLA Ops:
  0.6 0.7 convert_element_type.3
  1.3 0.8 multiply_sine_fusion.1
  2.2 0.5 fusion
  2.7 1.0 pad_maximum_fusion
  3.7 35.3 %front0.1 = (bf16[256,256]{1,0:T(8,128)(2,1)}, bf16[256,256]{1,0:T(8,128)(2,1)}, bf16[4,256,256]{2,1,0:T(8,128)(2,1)}, bf16[64,128,256]{2,1,0:T(8,128)(2,1)}, f32[256,2048]{1,0:T(8,128)}) custom-call(bf16[256,2048]{1,0:T(8,128)(2,1)} %x_ref.3, bf16[2,2048]{1,0:T(2,128)(2,1)} %gain_ref.3, f32[256,128]{1,0:T(8,128)} %get-tuple-element.28.cos_ref, ...), custom_call_target="tpu_custom_call" | custom-call | tf_op jit(solution)/shard_map/front0/pallas_call | solution.py:443
  39.0 60.9 %attn.2.o_ref = bf16[4,256,256]{2,1,0:T(8,128)(2,1)} custom-call(bf16[4,256,256]{2,1,0:T(8,128)(2,1)} %get-tuple-element.13.q_ref, bf16[64,128,256]{2,1,0:T(8,128)(2,1)} %get-tuple-element.14.kv_ref), custom_call_target="tpu_custom_call" | custom-call | tf_op jit(solution)/shard_map/attn/pallas_call | solution.py:456
  99.8 21.3 %back0.1.x_ref = bf16[256,2048]{1,0:T(8,128)(2,1)} custom-call(bf16[4,256,256]{2,1,0:T(8,128)(2,1)} %attn.2.o_ref, f32[256,2048]{1,0:T(8,128)} %get-tuple-element.15.mlp_ref, bf16[256,2048]{1,0:T(8,128)(2,1)} %x_ref.3, bf16[2,1024,2048]{2,1,0:T(8,128)(2,1)} %bitcast.20), custom_call_target="tpu_custom_call" | custom-call | tf_op jit(solution)/shard_map/back0/pallas_call | solution.py:465
  121.2 34.7 %front1.1 = (bf16[256,256]{1,0:T(8,128)(2,1)}, bf16[256,256]{1,0:T(8,128)(2,1)}, bf16[4,256,256]{2,1,0:T(8,128)(2,1)}, bf16[64,128,256]{2,1,0:T(8,128)(2,1)}, f32[256,2048]{1,0:T(8,128)}) custom-call(bf16[256,2048]{1,0:T(8,128)(2,1)} %back0.1.x_ref, bf16[2,2048]{1,0:T(2,128)(2,1)} %gain_ref.3, f32[256,128]{1,0:T(8,128)} %get-tuple-element.28.cos_ref, ...), custom_call_target="tpu_custom_call" | custom-call | tf_op jit(solution)/shard_map/front1/pallas_call | solution.py:443
  155.9 60.9 %attn.3.o_ref = bf16[4,256,256]{2,1,0:T(8,128)(2,1)} custom-call(bf16[4,256,256]{2,1,0:T(8,128)(2,1)} %get-tuple-element.16.q_ref, bf16[64,128,256]{2,1,0:T(8,128)(2,1)} %get-tuple-element.17.kv_ref), custom_call_target="tpu_custom_call" | custom-call | tf_op jit(solution)/shard_map/attn/pallas_call | solution.py:456
  216.8 0.0 copy-start.1
  216.8 0.0 copy-start.3
  216.8 0.0 copy-start
  216.8 0.0 copy-start.2
  216.8 21.3 %back1.1 = bf16[256,2048]{1,0:T(8,128)(2,1)} custom-call(bf16[4,256,256]{2,1,0:T(8,128)(2,1)} %attn.3.o_ref, f32[256,2048]{1,0:T(8,128)} %get-tuple-element.18.mlp_ref, bf16[256,2048]{1,0:T(8,128)(2,1)} %back0.1.x_ref, bf16[2,1024,2048]{2,1,0:T(8,128)(2,1)} %bitcast.21), custom_call_target="tpu_custom_call" | custom-call | tf_op jit(solution)/shard_map/back1/pallas_call | solution.py:465
  238.1 0.0 copy-done.1
  238.1 0.0 copy-done.3
  238.1 0.7 maximum_bitcast_fusion
  238.8 0.0 copy-done
  238.8 0.0 copy-done.2
  238.8 0.7 maximum_bitcast_fusion.1
  239.6 2.3 copy.15
  (1 shorter events, 0.0 us)
Async XLA Ops:
  216.8 21.3 %copy-start.1 = (bf16[256,256]{1,0:T(8,128)(2,1)S(1)}, bf16[256,256]{1,0:T(8,128)(2,1)}, u32[]{:S(2)}) copy-start(bf16[256,256]{1,0:T(8,128)(2,1)} %get-tuple-element.19) | copy-start | bytes 393220
  216.8 21.3 %copy-start.3 = (bf16[256,256]{1,0:T(8,128)(2,1)S(1)}, bf16[256,256]{1,0:T(8,128)(2,1)}, u32[]{:S(2)}) copy-start(bf16[256,256]{1,0:T(8,128)(2,1)} %get-tuple-element.20) | copy-start | bytes 393220
  216.8 22.0 %copy-start = (bf16[256,256]{1,0:T(8,128)(2,1)S(1)}, bf16[256,256]{1,0:T(8,128)(2,1)}, u32[]{:S(2)}) copy-start(bf16[256,256]{1,0:T(8,128)(2,1)} %get-tuple-element.21) | copy-start | bytes 393220
  216.8 22.0 %copy-start.2 = (bf16[256,256]{1,0:T(8,128)(2,1)S(1)}, bf16[256,256]{1,0:T(8,128)(2,1)}, u32[]{:S(2)}) copy-start(bf16[256,256]{1,0:T(8,128)(2,1)} %get-tuple-element.22) | copy-start | bytes 393220

commit v2 on v0

v2 whole, which is shorter than its diff:
```python
import functools
import jax
import jax.numpy as jnp
from jax import lax
from jax.experimental import pallas as pl
from jax.experimental.pallas import tpu as pltpu
from jax.sharding import PartitionSpec as P

ROPE_BASE = 500000.0
EPS = 1e-5
LOG2E = 1.4426950408889634
NEG = -1e30
MESH = pl.DeviceIdType.MESH
TOK, DM, QW, LN, HD = 256, 2048, 1024, 128, 64
F32 = jnp.float32
BF16 = jnp.bfloat16
VMEM_LIMIT = 62 * 1024 * 1024

DIM_ORDER = (((0, 1, 2), (0, 1, 2), (1, 2, 0), (2, 0, 1)), ((0, 1, 2), (1, 2, 0), (1, 2, 0), (2, 0, 1)))


def rope_tables(positions, head_dim):
    half_dim = head_dim // 2
    inv_freq = ROPE_BASE ** (-(jnp.arange(half_dim, dtype=F32) * 2.0 / head_dim))
    angles = positions.astype(F32)[None, :] * inv_freq[:, None]
    return jnp.cos(angles), jnp.sin(angles)


class Place:
    def __init__(self):
        self.seq = lax.axis_index('seq')
        self.head = lax.axis_index('head')
        self.xyz = (self.seq % 4, (self.seq // 4) % 4, self.seq // 16)
        self.mem = tuple(c // 2 for c in self.xyz)
        self.cls = tuple(((c + 1) // 2) % 2 for c in self.xyz)
        self.core = (self.mem[0] + self.mem[1]) % 2
        self.kv_local = 2 * self.mem[1] + self.mem[0]
        self.member = 2 * self.mem[2] + self.mem[0]

    def is_self(self):
        same_z = 1 - lax.rem(self.head + self.mem[2], 2)
        same_c = 1 - lax.rem(self.head + self.core, 2)
        return same_z * same_c

    def at(self, mem, cls):
        cs = [m * 3 + c * (1 - 2 * m) for m, c in zip(mem, cls)]
        return cs[2] * 16 + cs[1] * 4 + cs[0]

    def target(self, t):
        return self.at((t % 2, t // 2, self.head), self.cls)

    def source_mem(self, i):
        mx, mz = i % 2, i // 2
        return (mx, (mx + self.head) % 2, mz)

    def source(self, i, flips=()):
        cls = [1 - c if d in flips else c for d, c in enumerate(self.cls)]
        return self.at(self.source_mem(i), cls)

    def partner(self, dim):
        cls = [1 - c if d == dim else c for d, c in enumerate(self.cls)]
        return self.at(self.mem, cls)

    def dev(self, seq, head):
        return {'seq': seq, 'head': head}


N_TILES = 16
N_BEFORE = 14
NB = 4
TK = NB * TOK
HALF = NB * LN
RC = 16
NT = (((1,), (1,)), ((), ()))


def fold_max(x):
    return jnp.max(x.reshape(x.shape[0] // RC, RC, x.shape[1]), axis=0)


def fold_sum(x):
    return jnp.sum(x.reshape(x.shape[0] // RC, RC, x.shape[1]), axis=0)


def attn_logits(first, c, kv_all, qa, qb, sbuf, off, mx_ref, moff):
    cols = pl.ds(c * TOK, TOK)
    keys = kv_all[pl.ds(first, NB), 0:LN, :].reshape(HALF, LN)
    sa = jnp.dot(keys, qa[:, cols], preferred_element_type=F32) * (LOG2E / 8.0)
    sb = jnp.dot(keys, qb[:, cols], preferred_element_type=F32) * (LOG2E / 8.0)
    sbuf[pl.ds(off, HALF), cols] = sa
    sbuf[pl.ds(off + HALF, HALF), cols] = sb
    mx_ref[pl.ds(moff, RC), cols] = jnp.maximum(fold_max(sa), fold_max(sb))


def attn_update(cols, mx, parts, vTs, m_ref, l_ref, acc_ref):
    m_old = m_ref[0:1, cols]
    m_new = jnp.maximum(m_old, jnp.max(mx, axis=0, keepdims=True))
    alpha = jnp.exp2(m_old - m_new)
    m_ref[:, cols] = jnp.broadcast_to(m_new, (8, TOK))
    lsum = l_ref[:, cols] * alpha
    ps = []
    for s in parts:
        p = jnp.exp2(s - m_new)
        lsum = lsum + fold_sum(p)
        ps.append(p.astype(BF16))
    l_ref[:, cols] = lsum
    pv = jnp.dot(jnp.concatenate(vTs, axis=1), jnp.concatenate(ps, axis=0), preferred_element_type=F32)
    acc_ref[:, cols] = acc_ref[:, cols] * alpha + pv


def values_of(kv_all, first, blocks):
    return [kv_all[first + b, LN + HD * h:192 + HD * h, :] for h in range(2) for b in range(blocks)]


def attn_tail(first, t, kv_all, sbuf, off, m_ref, l_ref, acc_ref):
    def col(c, carry):
        cols = pl.ds(pl.multiple_of(c * TOK, TOK), TOK)
        ti = lax.broadcasted_iota(jnp.int32, (LN, TOK), 1)
        ki = lax.broadcasted_iota(jnp.int32, (LN, TOK), 0)
        parts = []
        for h in range(2):
            base = pl.multiple_of(off + h * HALF, LN)
            if t > 0:
                parts.append(sbuf[pl.ds(base, t * LN), cols])
            parts.append(jnp.where(ki + h * LN <= ti, sbuf[pl.ds(base + t * LN, LN), cols], NEG))
        mx = functools.reduce(jnp.maximum, [fold_max(p) for p in parts])
        attn_update(cols, mx, parts, values_of(kv_all, first, t + 1), m_ref, l_ref, acc_ref)
        return carry

    lax.fori_loop(0, 4, col, 0)


def attn_block(pos, qT, kv_all, store, qa, qb, m_ref, l_ref, acc_ref, sbuf, mx_ref):
    zero = jnp.zeros((HD, TOK), BF16)
    for g in range(4):
        q = qT[g * HD:(g + 1) * HD, :]
        cols = pl.ds(g * TOK, TOK)
        qa[:, cols] = jnp.concatenate([q, zero], axis=0)
        qb[:, cols] = jnp.concatenate([zero, q], axis=0)
    m_ref[:] = jnp.full_like(m_ref, NEG)
    l_ref[:] = jnp.zeros_like(l_ref)
    acc_ref[:] = jnp.zeros_like(acc_ref)
    groups = pos // NB
    for c in range(4):
        attn_logits(0, c, kv_all, qa, qb, sbuf, 0, mx_ref, 0)

    def one(n, p):
        for c in range(4):
            attn_logits((n + 1) * NB, c, kv_all, qa, qb, sbuf, (1 - p) * TK, mx_ref, (1 - p) * RC)
            cols = pl.ds(c * TOK, TOK)
            attn_update(cols, mx_ref[pl.ds(p * RC, RC), cols], [sbuf[pl.ds(p * TK, TK), cols]], values_of(kv_all, n * NB, NB), m_ref, l_ref, acc_ref)

    def pair(i, carry):
        one(2 * i, 0)
        one(2 * i + 1, 1)
        return carry

    lax.fori_loop(0, groups // 2, pair, 0)

    @pl.when(groups % 2 == 1)
    def _():
        one(groups - 1, 0)
    for t in range(NB):
        @pl.when(pos % NB == t)
        def _():
            attn_tail(groups * NB, t, kv_all, sbuf, (groups % 2) * TK, m_ref, l_ref, acc_ref)
    oT = acc_ref[:] / jnp.sum(l_ref[:], axis=0, keepdims=True)
    halves = []
    for g in range(0, 4, 2):
        two = jnp.concatenate([oT[:, g * TOK:(g + 1) * TOK], oT[:, (g + 1) * TOK:(g + 2) * TOK]], axis=0)
        halves.append(two.T.astype(BF16))
    store(jnp.concatenate(halves, axis=1))


def layer_kernel(layer, x_ref, gain_ref, cosT_ref, sinT_ref, wq, wk, wv, wg, wu, wd, wo, out_ref, kT_ref, vT_ref,
                 h_ref, q_send, kv_send, q_all, kv_all, o_send, o_full, mlp, part, part_in, wqb, wkb, wvb, wgb, wub, wdb, wob,
                 qa, qb, m_ref, l_ref, acc_ref, sbuf, mx_ref,
                 wsem, msem, osem, skv, sq, sag, sdd, so, sp, rkv, rq, rag, rdd, ro, rp):
    me = Place()
    sib = 1 - me.head
    flag = me.is_self()

    def s_self(i):
        return flag * (1 - lax.rem(i // 2 + me.mem[2], 2)) * (1 - lax.rem(i % 2 + me.mem[0], 2))

    def t_self(t):
        return flag * (1 - lax.rem(t // 2 + me.mem[1], 2)) * (1 - lax.rem(t % 2 + me.mem[0], 2))

    def remote(src, dst, ssem, rsem, seq, head):
        return pltpu.make_async_remote_copy(src_ref=src, dst_ref=dst, send_sem=ssem, recv_sem=rsem, device_id=me.dev(seq, head), device_id_type=MESH)

    barrier = pltpu.get_barrier_semaphore()
    for i in range(4):
        @pl.when(s_self(i) == 0)
        def _():
            pl.semaphore_signal(barrier, inc=1, device_id=me.dev(me.source(i), me.mem[2]), device_id_type=MESH)
    for t in range(4):
        @pl.when(t_self(t) == 0)
        def _():
            pl.semaphore_signal(barrier, inc=1, device_id=me.dev(me.target(t), me.core), device_id_type=MESH)
    for d in range(3):
        pl.semaphore_signal(barrier, inc=1, device_id=me.dev(me.partner(d), me.head), device_id_type=MESH)
    pl.semaphore_signal(barrier, inc=1, device_id=me.dev(me.seq, sib), device_id_type=MESH)

    cps = [pltpu.make_async_copy(wk.at[layer], wkb, wsem.at[0]), pltpu.make_async_copy(wv.at[layer], wvb, wsem.at[1])]
    for t in range(4):
        cps.append(pltpu.make_async_copy(wq.at[layer, pl.ds(t * TOK, TOK)], wqb.at[t], wsem.at[2 + t]))
    for c in cps:
        c.start()

    def tile_copies(n, slot):
        off = pl.multiple_of(n * TOK, TOK)
        return (pltpu.make_async_copy(wg.at[layer, :, pl.ds(off, TOK)], wgb.at[slot], msem.at[slot, 0]),
                pltpu.make_async_copy(wu.at[layer, :, pl.ds(off, TOK)], wub.at[slot], msem.at[slot, 1]),
                pltpu.make_async_copy(wd.at[layer, pl.ds(off, TOK)], wdb.at[slot], msem.at[slot, 2]))

    for n in range(3):
        for c in tile_copies(n, n):
            c.start()
    wo_cps = [pltpu.make_async_copy(wo.at[layer, pl.ds(t * TOK, TOK)], wob.at[t], osem.at[t]) for t in range(4)]

    xf = x_ref[:].astype(F32)
    inv = lax.rsqrt(jnp.mean(xf * xf, axis=-1, keepdims=True) + EPS)
    h_ref[:] = (xf * inv * gain_ref[layer:layer + 1, :].astype(F32)).astype(BF16)

    cosT, sinT = cosT_ref[:], sinT_ref[:]

    def rope(a):
        lo, hi = a[0:32], a[32:HD]
        return jnp.concatenate([lo * cosT - hi * sinT, hi * cosT + lo * sinT], axis=0)

    def project(w):
        return lax.dot_general(w, h_ref[:], NT, preferred_element_type=F32).astype(BF16)

    cps[0].wait()
    kT = project(wkb[:]).astype(F32)
    for t in range(4):
        k = rope(kT[t * HD:(t + 1) * HD]).astype(BF16)
        kT_ref[t * HD:(t + 1) * HD, :] = k
        kf = k.astype(F32)
        kv_send[t, 0:LN, :] = jnp.concatenate([kf[:, 0:LN], kf[:, LN:TOK]], axis=0).T.astype(BF16)
    cps[1].wait()
    vT = project(wvb[:])
    vT_ref[:] = vT
    for t in range(4):
        kv_send[t, LN:192, :] = vT[t * HD:(t + 1) * HD, 0:LN]
        kv_send[t, 192:TOK, :] = vT[t * HD:(t + 1) * HD, LN:TOK]

    pl.semaphore_wait(barrier, 12 - 2 * flag)

    def kv_copy(t):
        return remote(kv_send.at[t], kv_all.at[me.seq], skv.at[t], rkv.at[me.member], me.target(t), me.core)

    def q_copy(t):
        return remote(q_send.at[t], q_all.at[me.member], sq.at[t], rq.at[me.member], me.target(t), me.core)

    def send_all(make, src, dst, idx):
        for t in range(4):
            @pl.when(t_self(t) == 0)
            def _():
                make(t).start()

            @pl.when(t_self(t) == 1)
            def _():
                dst[idx] = src[t]

    send_all(kv_copy, kv_send, kv_all, me.seq)

    for t in range(4):
        cps[2 + t].wait()
        qT = project(wqb[t]).astype(F32)
        for g in range(4):
            q_send[t, g * HD:(g + 1) * HD, :] = rope(qT[g * HD:(g + 1) * HD]).astype(BF16)
    send_all(q_copy, q_send, q_all, me.member)

    def plan(core, i, k):
        d1, d2, d3 = DIM_ORDER[core][i]
        return ((d1, ()), (d2, ()), (d2, (d1,)), (d3, ()), (d3, (d1,)), (d3, (d2,)), (d3, (d1, d2)))[k]

    def got(core, i, k):
        dim, flips = plan(core, i, k)
        return tuple(flips) + (dim,)

    def ag(core, i, k):
        dim, flips = plan(core, i, k)
        block = kv_all.at[me.source(i, flips)]
        return remote(block, block, sag.at[i, k], rag.at[i, k], me.partner(dim), me.head)

    def ag_recv(core, i, k):
        block = kv_all.at[me.source(i, got(core, i, k))]
        remote(block, block, sag.at[i, k], rag.at[i, k], me.seq, sib).wait_recv()

    def dd(pos, i, k):
        return remote(kv_all.at[pos], kv_all.at[pos], sdd.at[i, k], rdd.at[i, k], me.seq, sib)

    def relay(core, i, k):
        dd(me.source(i, got(core, i, k)), i, k + 1).start()

    def per_core(fn, *a):
        for core in range(2):
            @pl.when(me.head == core)
            def _():
                fn(core, *a)

    def step1(core, group):
        for i in group:
            @pl.when(s_self(i) == 0)
            def _():
                remote(kv_send.at[0], kv_all.at[me.source(i)], skv.at[0], rkv.at[i], me.seq, sib).wait_recv()
            ag(core, i, 0).start()
        for k in (1, 3):
            for i in group:
                ag(core, i, k).start()
        for i in group:
            dd(me.source(i), i, 0).start()

    def step2(core, group):
        for i in group:
            ag_recv(core, i, 0)
            ag(core, i, 2).start()
            ag(core, i, 4).start()
            relay(core, i, 0)
        for i in group:
            ag_recv(core, i, 1)
            ag(core, i, 5).start()
            relay(core, i, 1)

    def step3(core, group):
        for i in group:
            ag_recv(core, i, 2)
            ag(core, i, 6).start()
            relay(core, i, 2)

    def step4(core, group):
        for k in range(3, 7):
            for i in group:
                ag_recv(core, i, k)
                relay(core, i, k)

    def sibling_blocks(core, group):
        other = 1 - core
        for k in range(8):
            for i in group:
                mx, mz = i % 2, i // 2
                flips = () if k == 0 else got(other, i, k - 1)
                cls = [1 - c if d in flips else c for d, c in enumerate(me.cls)]
                dd(me.at((mx, (mx + other) % 2, mz), cls), i, k).wait_recv()

    mlp[:] = jnp.zeros_like(mlp)
    low, high = (0, 1), (2, 3)
    events = EVENTS

    def tile(n, carry):
        slot = n % 3
        for c in tile_copies(n, slot):
            c.wait()
        for at, name, group in events:
            @pl.when(n == at)
            def _():
                per_core({1: step1, 2: step2, 3: step3, 4: step4}[name], group)
        g = jnp.dot(h_ref[:], wgb[slot], preferred_element_type=F32)
        u = jnp.dot(h_ref[:], wub[slot], preferred_element_type=F32)
        hid = (g * jax.nn.sigmoid(g) * u).astype(BF16)
        mlp[:] += jnp.dot(hid, wdb[slot], preferred_element_type=F32)

        @pl.when(n + 3 < N_TILES)
        def _():
            for c in tile_copies(n + 3, slot):
                c.start()
        return carry

    lax.fori_loop(0, N_BEFORE, tile, 0)
    for c in wo_cps:
        c.start()
    per_core(step4, low)
    per_core(sibling_blocks, low)
    for i in range(4):
        @pl.when(s_self(i) == 0)
        def _():
            remote(q_send.at[0], q_all.at[i], sq.at[0], rq.at[i], me.seq, sib).wait_recv()

    def o_copy(i):
        return remote(o_send.at[i], o_full.at[me.kv_local], so.at[i], ro.at[me.kv_local], me.source(i), me.mem[2])

    def query(n, carry):
        first = (1 - n % 2) * me.head + (n % 2) * (1 - me.head)
        i = 2 * (n // 2) + first

        @pl.when(n == 2)
        def _():
            per_core(sibling_blocks, high)

        def store(val):
            o_send[i] = val
        attn_block(me.source(i), q_all[i], kv_all, store, qa, qb, m_ref, l_ref, acc_ref, sbuf, mx_ref)

        @pl.when(n == 0)
        def _():
            per_core(step4, high)
        own = s_self(i)

        @pl.when(own == 0)
        def _():
            o_copy(i).start()

        @pl.when(own == 1)
        def _():
            o_full[me.kv_local] = o_send[i]
        return carry

    lax.fori_loop(0, 4, query, 0)
    lax.fori_loop(N_BEFORE, N_TILES, tile, 0)

    for c in wo_cps:
        c.wait()
    for t in range(4):
        @pl.when(t_self(t) == 0)
        def _():
            remote(o_send.at[0], o_full.at[t], so.at[0], ro.at[t], me.seq, sib).wait_recv()

    def p_copy(n):
        return remote(part.at[n], part_in.at[n], sp.at[n], rp.at[n], me.seq, sib)

    for n in range(8):
        cols = pl.ds(n * TOK, TOK)
        heads = jnp.concatenate([o_full[t] for t in range(4)], axis=1)
        w = jnp.concatenate([wob[t, :, cols] for t in range(4)], axis=0)
        part[n] = mlp[:, cols] + jnp.dot(heads, w, preferred_element_type=F32)
        p_copy(n).start()
    for n in range(8):
        cols = pl.ds(n * TOK, TOK)
        p_copy(n).wait_recv()
        y = (part[n] + part_in[n]).astype(BF16)
        out_ref[:, cols] = (x_ref[:, cols].astype(F32) + y.astype(F32)).astype(BF16)

    for t in range(4):
        @pl.when(t_self(t) == 0)
        def _():
            kv_copy(t).wait_send()
            q_copy(t).wait_send()

    def sent(core):
        for i in range(4):
            for k in range(7):
                ag(core, i, k).wait_send()
            for k in range(8):
                dd(me.source(i), i, k).wait_send()
    per_core(sent)
    for i in range(4):
        @pl.when(s_self(i) == 0)
        def _():
            o_copy(i).wait_send()
    for n in range(8):
        p_copy(n).wait_send()


EVENTS = ((3, 1, (0, 1)), (6, 2, (0, 1)), (6, 1, (2, 3)), (9, 3, (0, 1)), (9, 2, (2, 3)), (12, 3, (2, 3)))


SCRATCH = [
    pltpu.VMEM((TOK, DM), BF16), pltpu.VMEM((4, TOK, TOK), BF16), pltpu.VMEM((4, TOK, LN), BF16),
    pltpu.VMEM((4, TOK, TOK), BF16), pltpu.VMEM((HD, TOK, LN), BF16), pltpu.VMEM((4, TOK, TOK), BF16), pltpu.VMEM((4, TOK, TOK), BF16),
    pltpu.VMEM((TOK, DM), F32), pltpu.VMEM((8, TOK, TOK), F32), pltpu.VMEM((8, TOK, TOK), F32),
    pltpu.VMEM((4, TOK, DM), BF16), pltpu.VMEM((TOK, DM), BF16), pltpu.VMEM((TOK, DM), BF16),
    pltpu.VMEM((3, DM, TOK), BF16), pltpu.VMEM((3, DM, TOK), BF16), pltpu.VMEM((3, TOK, DM), BF16), pltpu.VMEM((4, TOK, DM), BF16),
    pltpu.VMEM((LN, QW), BF16), pltpu.VMEM((LN, QW), BF16), pltpu.VMEM((8, QW), F32), pltpu.VMEM((RC, QW), F32), pltpu.VMEM((HD, QW), F32),
    pltpu.VMEM((2 * TK, QW), F32), pltpu.VMEM((2 * RC, QW), F32),
] + [pltpu.SemaphoreType.DMA(s) for s in ((6,), (3, 3), (4,), (4,), (4,), (4, 7), (4, 8), (4,), (8,), (4,), (4,), (4, 7), (4, 8), (4,), (8,))]


def vm():
    return pl.BlockSpec(memory_space=pltpu.VMEM)


def hbm():
    return pl.BlockSpec(memory_space=pl.ANY)


def sds(shape, dtype):
    return jax.ShapeDtypeStruct(shape, dtype)


def dma(*shape):
    return pltpu.SemaphoreType.DMA(shape)


def solution(mesh):
    row_spec = P(('batch', 'seq'), None)
    pos_spec = P(('batch', 'seq'))
    head_spec = P(None, None, 'head', None)
    out_proj_spec = P(None, 'head', None, None)
    col_spec = P(None, None, 'head')
    down_spec = P(None, 'head', None)
    cache_spec = P(None, ('batch', 'seq'), 'head', None)

    def local_forward(x, pos, w_q, w_k, w_v, w_o, w_gate, w_up, w_down, gain):
        cosT, sinT = rope_tables(pos, HD)
        wq = w_q.transpose(0, 2, 3, 1).reshape(2, QW, DM)
        wk = w_k.transpose(0, 2, 3, 1).reshape(2, TOK, DM)
        wv = w_v.transpose(0, 2, 3, 1).reshape(2, TOK, DM)
        wo = w_o.reshape(2, QW, DM)
        ks, vs = [], []
        for layer in range(2):
            x, kT, vT = pl.pallas_call(
                functools.partial(layer_kernel, layer),
                out_shape=(sds((TOK, DM), BF16), sds((TOK, TOK), BF16), sds((TOK, TOK), BF16)),
                in_specs=[vm()] * 4 + [hbm()] * 7,
                out_specs=[vm()] * 3,
                scratch_shapes=SCRATCH,
                compiler_params=pltpu.CompilerParams(collective_id=layer, has_side_effects=True, vmem_limit_bytes=VMEM_LIMIT),
                name=f'layer{layer}',
            )(x, gain, cosT, sinT, wq, wk, wv, w_gate, w_up, w_down, wo)
            ks.append(kT)
            vs.append(vT)
        k_cache = jnp.stack(ks).reshape(2, 4, HD, TOK).transpose(0, 3, 1, 2)
        v_cache = jnp.stack(vs).reshape(2, 4, HD, TOK).transpose(0, 3, 1, 2)
        return x, k_cache, v_cache

    return jax.shard_map(local_forward, mesh=mesh, in_specs=(row_spec, pos_spec, head_spec, head_spec, head_spec, out_proj_spec, col_spec, col_spec, down_spec, P(None, None)), out_specs=(row_spec, cache_spec, cache_spec), check_vma=False)
```

time: 1900 us -> 180 us (0.09)
  starting transfers between devices: 1220 us -> 0 us
  matrix products: 328 us -> 0 us
  Pallas kernels: 0 us -> 173 us
  other arithmetic: 136 us -> 3.33 us
  blocking collectives: 90.6 us -> 0 us
  local copies, waits for them, and re-layouts: 56.6 us -> 2.31 us
  waiting for transfers between devices: 45.9 us -> 0 us
    ppermute x252 -> x0, starting transfers between devices: 1220 us -> none  [the longest x126 879 us: pass_step(): v_blk = lax.ppermute(v_blk, 'seq', shift_pairs)]
    dot_general x268 -> x0, matrix products: 328 us -> none  [the longest x128 152 us: block_update(): jnp.einsum('qkgs,skd->qkgd', prob_f32.astype(jnp.bfloat16), v_blk, prefer...]
    pallas_call x0 -> x2, Pallas kernels: none -> 173 us  [local_forward(): pl.pallas_call(functools.partial(layer_kernel, layer), out_shape=(sds((TO...]
    reduce_sum x130 -> x0, other arithmetic: 115 us -> none  [the longest x128 113 us: block_update(): row_sum = row_sum * rescale + jnp.sum(prob_f32, axis=-1)]
    psum x2 -> x0, blocking collectives: 90.6 us -> none  [local_forward(): update = lax.psum(part_sum, 'head').astype(jnp.bfloat16)]
    ppermute x252 -> x0, waiting for transfers between devices: 45.9 us -> none  [the longest x126 30.2 us: pass_step(): v_blk = lax.ppermute(v_blk, 'seq', shift_pairs)]
    while x378 -> x0, local copies, waits for them, and re-layouts: 43.7 us -> none
  transfers between devices with their start and end apart: 252 -> 0, of which waited for: 70 -> 0; matrix products, arithmetic and copies ran while one was open for 14% -> 0% of each run, Pallas kernels for 0% -> 0%
where the time goes in v2:
time: 180 us; the launch traced here: 179 us
  Pallas kernels  173 us (96%)
  other arithmetic  3.33 us (2%)
  local copies, waits for them, and re-layouts  2.31 us (1%)
    pallas_call x2, Pallas kernels, local_forward(): pl.pallas_call(functools.partial(layer_kernel, layer), out_shape=(sds((TO...  173 us

profile of v2, /device:TPU:121, one launch (start us, length us, event | category | flops | bytes accessed | tf_op | source)
XLA Modules:
  0.0 178.9 jit_solution(10811954024045740884)
XLA Ops:
  0.6 0.7 convert_element_type.3
  1.3 0.8 multiply_sine_fusion
  2.2 87.6 %layer0.1 = (bf16[256,2048]{1,0:T(8,128)(2,1)}, bf16[256,256]{1,0:T(8,128)(2,1)}, bf16[256,256]{1,0:T(8,128)(2,1)}) custom-call(bf16[256,2048]{1,0:T(8,128)(2,1)} %x_ref.1, bf16[2,2048]{1,0:T(2,128)(2,1)} %gain_ref.3, f32[32,256]{1,0:T(8,128)} %get-tuple-element.16.cosT_ref, f32[32,256]{1,0:T(8,128)} %get-tuple-element.15.sinT_ref, ...), custom_call_target="tpu_custom_call" | custom-call | tf_op jit(solution)/shard_map/layer0/pallas_call | solution.py:504
  89.8 0.0 copy-start
  89.8 0.0 copy-start.1
  89.8 85.0 %layer1.1 = (bf16[256,2048]{1,0:T(8,128)(2,1)}, bf16[256,256]{1,0:T(8,128)(2,1)}, bf16[256,256]{1,0:T(8,128)(2,1)}) custom-call(bf16[256,2048]{1,0:T(8,128)(2,1)} %get-tuple-element.9.x_ref, bf16[2,2048]{1,0:T(2,128)(2,1)} %gain_ref.3, f32[32,256]{1,0:T(8,128)} %get-tuple-element.16.cosT_ref, f32[32,256]{1,0:T(8,128)} %get-tuple-element.15.sinT_ref, ...), custom_call_target="tpu_custom_call" | custom-call | tf_op jit(solution)/shard_map/layer1/pallas_call | solution.py:504
  174.8 0.0 copy-done
  174.8 0.0 copy-done.1
  174.8 1.8 %maximum_bitcast_fusion = (bf16[2,256,4,64]{1,3,2,0:T(8,128)(2,1)}, bf16[2,256,4,64]{1,3,2,0:T(8,128)(2,1)}) fusion(bf16[1,4,64,256]{3,2,1,0:T(8,128)(2,1)} %bitcast.28, bf16[1,4,64,256]{3,2,1,0:T(8,128)(2,1)S(1)} %bitcast.26, bf16[1,4,64,256]{3,2,1,0:T(8,128)(2,1)} %bitcast.29, bf16[1,4,64,256]{3,2,1,0:T(8,128)(2,1)S(1)} %bitcast.27), kind=kLoop, calls=%fused_computation | loop fusion | flops 262144 | bytes 1048576 | tf_op jit(solution)/shard_map/transpose | solution.py:515
  176.6 2.3 %copy.14 = bf16[256,2048]{1,0:T(8,128)(2,1)} copy(bf16[256,2048]{1,0:T(8,128)(2,1)} %get-tuple-element.22) | data formatting | bytes 2097152
  (1 shorter events, 0.0 us)
Async XLA Ops:
  89.8 85.0 %copy-start = (bf16[256,256]{1,0:T(8,128)(2,1)S(1)}, bf16[256,256]{1,0:T(8,128)(2,1)}, u32[]{:S(2)}) copy-start(bf16[256,256]{1,0:T(8,128)(2,1)} %get-tuple-element.11) | copy-start | bytes 393220
  89.8 85.0 %copy-start.1 = (bf16[256,256]{1,0:T(8,128)(2,1)S(1)}, bf16[256,256]{1,0:T(8,128)(2,1)}, u32[]{:S(2)}) copy-start(bf16[256,256]{1,0:T(8,128)(2,1)} %get-tuple-element.13) | copy-start | bytes 393220

commit v3 on v0

v3 whole, which is shorter than its diff:
```python
import functools
import jax
import jax.numpy as jnp
from jax import lax
from jax.experimental import pallas as pl
from jax.experimental.pallas import tpu as pltpu
from jax.sharding import PartitionSpec as P

ROPE_BASE = 500000.0
EPS = 1e-5
LOG2E = 1.4426950408889634
NEG = -1e30
MESH = pl.DeviceIdType.MESH
TOK, DM, QW, LN, HD = 256, 2048, 1024, 128, 64
F32 = jnp.float32
BF16 = jnp.bfloat16
VMEM_LIMIT = 62 * 1024 * 1024

STRIDE = (1, 4, 16)
N_TILES = 16
LAST_BEFORE = 14
NB = 4
TK = NB * TOK
HALF = NB * LN
RC = 16
NT = (((1,), (1,)), ((), ()))
LOW, HIGH = (0, 1), (2, 3)
SENDS = ((0, ()), (1, ()), (1, (0,)), (2, ()), (2, (0,)), (2, (1,)), (2, (0, 1)))


def rope_tables(positions, head_dim):
    half_dim = head_dim // 2
    inv_freq = ROPE_BASE ** (-(jnp.arange(half_dim, dtype=F32) * 2.0 / head_dim))
    angles = positions.astype(F32)[None, :] * inv_freq[:, None]
    return jnp.cos(angles), jnp.sin(angles)


class Place:
    def __init__(self):
        self.seq = lax.axis_index('seq')
        self.head = lax.axis_index('head')
        self.xyz = (self.seq % 4, (self.seq // 4) % 4, self.seq // 16)
        self.mem = tuple(c // 2 for c in self.xyz)
        self.cls = tuple(((c + 1) // 2) % 2 for c in self.xyz)
        self.core = (self.mem[0] + self.mem[1]) % 2
        self.kv_local = 2 * self.mem[1] + self.mem[0]
        self.member = 2 * self.mem[2] + self.mem[0]
        same_z = 1 - lax.rem(self.head + self.mem[2], 2)
        self.flag = same_z * (1 - lax.rem(self.head + self.core, 2))

    def at(self, mem):
        cs = [m * 3 + c * (1 - 2 * m) for m, c in zip(mem, self.cls)]
        return cs[2] * 16 + cs[1] * 4 + cs[0]

    def target(self, t):
        return self.at((t % 2, t // 2, self.head))

    def source_mem(self, i):
        mx = i % 2
        return (mx, (mx + self.head) % 2, i // 2)

    def source(self, i):
        return self.at(self.source_mem(i))

    def steps(self, i, mem):
        d = [(1 - 2 * c) * (1 - 2 * m) * s for c, m, s in zip(self.cls, mem, STRIDE)]
        turns = [d[k:] + d[:k] for k in range(3)]
        if i == 1:
            return [a * (1 - self.head) + b * self.head for a, b in zip(turns[0], turns[1])]
        return turns[max(i - 1, 0)]

    def s_self(self, i):
        return self.flag * (1 - lax.rem(i // 2 + self.mem[2], 2)) * (1 - lax.rem(i % 2 + self.mem[0], 2))

    def t_self(self, t):
        return self.flag * (1 - lax.rem(t // 2 + self.mem[1], 2)) * (1 - lax.rem(t % 2 + self.mem[0], 2))


def fold_max(x):
    return jnp.max(x.reshape(x.shape[0] // RC, RC, x.shape[1]), axis=0)


def fold_sum(x):
    return jnp.sum(x.reshape(x.shape[0] // RC, RC, x.shape[1]), axis=0)


def attn_logits(first, c, kv_all, qa, qb, sbuf, off, mx_ref, moff):
    cols = pl.ds(c * TOK, TOK)
    keys = kv_all[pl.ds(first, NB), 0:LN, :].reshape(HALF, LN)
    sa = jnp.dot(keys, qa[:, cols], preferred_element_type=F32) * (LOG2E / 8.0)
    sb = jnp.dot(keys, qb[:, cols], preferred_element_type=F32) * (LOG2E / 8.0)
    sbuf[pl.ds(off, HALF), cols] = sa
    sbuf[pl.ds(off + HALF, HALF), cols] = sb
    mx_ref[pl.ds(moff, RC), cols] = jnp.maximum(fold_max(sa), fold_max(sb))


def attn_update(cols, mx, parts, vTs, m_ref, l_ref, acc_ref):
    m_old = m_ref[0:1, cols]
    m_new = jnp.maximum(m_old, jnp.max(mx, axis=0, keepdims=True))
    alpha = jnp.exp2(m_old - m_new)
    m_ref[:, cols] = jnp.broadcast_to(m_new, (8, TOK))
    lsum = l_ref[:, cols] * alpha
    ps = []
    for s in parts:
        p = jnp.exp2(s - m_new)
        lsum = lsum + fold_sum(p)
        ps.append(p.astype(BF16))
    l_ref[:, cols] = lsum
    pv = jnp.dot(jnp.concatenate(vTs, axis=1), jnp.concatenate(ps, axis=0), preferred_element_type=F32)
    acc_ref[:, cols] = acc_ref[:, cols] * alpha + pv


def values_of(kv_all, first, blocks):
    return [kv_all[first + b, LN + HD * h:192 + HD * h, :] for h in range(2) for b in range(blocks)]


def attn_tail(first, t, kv_all, sbuf, off, m_ref, l_ref, acc_ref):
    def col(c, carry):
        cols = pl.ds(pl.multiple_of(c * TOK, TOK), TOK)
        ti = lax.broadcasted_iota(jnp.int32, (LN, TOK), 1)
        ki = lax.broadcasted_iota(jnp.int32, (LN, TOK), 0)
        parts = []
        for h in range(2):
            base = pl.multiple_of(off + h * HALF, LN)
            if t > 0:
                parts.append(sbuf[pl.ds(base, t * LN), cols])
            parts.append(jnp.where(ki + h * LN <= ti, sbuf[pl.ds(base + t * LN, LN), cols], NEG))
        mx = functools.reduce(jnp.maximum, [fold_max(p) for p in parts])
        attn_update(cols, mx, parts, values_of(kv_all, first, t + 1), m_ref, l_ref, acc_ref)
        return carry

    lax.fori_loop(0, 4, col, 0)


def attn_block(pos, qT, kv_all, store, qa, qb, m_ref, l_ref, acc_ref, sbuf, mx_ref):
    zero = jnp.zeros((HD, TOK), BF16)
    for g in range(4):
        q = qT[g * HD:(g + 1) * HD, :]
        cols = pl.ds(g * TOK, TOK)
        qa[:, cols] = jnp.concatenate([q, zero], axis=0)
        qb[:, cols] = jnp.concatenate([zero, q], axis=0)
    m_ref[:] = jnp.full_like(m_ref, NEG)
    l_ref[:] = jnp.zeros_like(l_ref)
    acc_ref[:] = jnp.zeros_like(acc_ref)
    groups = pos // NB
    for c in range(4):
        attn_logits(0, c, kv_all, qa, qb, sbuf, 0, mx_ref, 0)

    def one(n, p):
        for c in range(4):
            attn_logits((n + 1) * NB, c, kv_all, qa, qb, sbuf, (1 - p) * TK, mx_ref, (1 - p) * RC)
            cols = pl.ds(c * TOK, TOK)
            attn_update(cols, mx_ref[pl.ds(p * RC, RC), cols], [sbuf[pl.ds(p * TK, TK), cols]], values_of(kv_all, n * NB, NB), m_ref, l_ref, acc_ref)

    def pair(i, carry):
        one(2 * i, 0)
        one(2 * i + 1, 1)
        return carry

    lax.fori_loop(0, groups // 2, pair, 0)

    @pl.when(groups % 2 == 1)
    def _():
        one(groups - 1, 0)
    for t in range(NB):
        @pl.when(pos % NB == t)
        def _():
            attn_tail(groups * NB, t, kv_all, sbuf, (groups % 2) * TK, m_ref, l_ref, acc_ref)
    oT = acc_ref[:] / jnp.sum(l_ref[:], axis=0, keepdims=True)
    halves = []
    for g in range(0, 4, 2):
        two = jnp.concatenate([oT[:, g * TOK:(g + 1) * TOK], oT[:, (g + 1) * TOK:(g + 2) * TOK]], axis=0)
        halves.append(two.T.astype(BF16))
    store(jnp.concatenate(halves, axis=1))


def stack_kernel(x_hbm, gain_ref, cos_hbm, sin_hbm, wq, wk, wv, wg, wu, wd, wo, x_ref, k_ref, v_ref,
                 cosT, sinT, h_ref, q_send, kv_send, q_all, kv_all, o_send, o_full, mlp, part_in, hid, wqb, wkvb, wgb, wub, wdb, wob,
                 qa, qb, m_ref, l_ref, acc_ref, sbuf, mx_ref,
                 xsem, wsem, msem, osem, skv, sq, sag, sdd, so, sp, rkv, rq, rag, rdd, ro, rp):
    me = Place()
    sib = 1 - me.head

    def remote(src, dst, ssem, rsem, seq, head):
        return pltpu.make_async_remote_copy(src_ref=src, dst_ref=dst, send_sem=ssem, recv_sem=rsem, device_id={'seq': seq, 'head': head}, device_id_type=MESH)

    def for_others(is_self, fn):
        for i in range(4):
            @pl.when(is_self(i) == 0)
            def _():
                fn(i)

    barrier = pltpu.get_barrier_semaphore()

    def hello(seq, head):
        pl.semaphore_signal(barrier, inc=1, device_id={'seq': seq, 'head': head}, device_id_type=MESH)

    for_others(me.s_self, lambda i: hello(me.source(i), me.mem[2]))
    for_others(me.t_self, lambda t: hello(me.target(t), me.core))
    for step in me.steps(0, me.mem):
        hello(me.seq + step, me.head)
    hello(me.seq, sib)

    start_cps = [pltpu.make_async_copy(x_hbm, x_ref, xsem.at[0]), pltpu.make_async_copy(cos_hbm, cosT, xsem.at[1]), pltpu.make_async_copy(sin_hbm, sinT, xsem.at[2])]

    def proj_copies(layer):
        return (pltpu.make_async_copy(wk.at[layer], wkvb.at[pl.ds(0, TOK)], wsem.at[0]), pltpu.make_async_copy(wv.at[layer], wkvb.at[pl.ds(TOK, TOK)], wsem.at[1]), pltpu.make_async_copy(wq.at[layer], wqb, wsem.at[2]))

    def gu_copies(layer, n):
        off = pl.multiple_of(n * TOK, TOK)
        slot = n % 3
        return (pltpu.make_async_copy(wg.at[layer, :, pl.ds(off, TOK)], wgb.at[slot], msem.at[0, slot]), pltpu.make_async_copy(wu.at[layer, :, pl.ds(off, TOK)], wub.at[slot], msem.at[1, slot]))

    def d_copy(layer, n):
        return pltpu.make_async_copy(wd.at[layer, pl.ds(pl.multiple_of(n * TOK, TOK), TOK)], wdb.at[n % 3], msem.at[2, n % 3])

    def first_tiles(layer):
        for n in range(3):
            for c in gu_copies(layer, n):
                c.start()
        for n in range(2):
            d_copy(layer, n).start()

    for c in start_cps:
        c.start()
    for c in proj_copies(0):
        c.start()
    first_tiles(0)
    for c in start_cps:
        c.wait()

    def rope(a):
        lo, hi = a[0:32], a[32:HD]
        return jnp.concatenate([lo * cosT[:] - hi * sinT[:], hi * cosT[:] + lo * sinT[:]], axis=0)

    def project(w):
        return lax.dot_general(w, h_ref[:], NT, preferred_element_type=F32).astype(BF16)

    def layer_body(layer, carry):
        kv = kv_all.at[layer]
        xf = x_ref[:].astype(F32)
        inv = lax.rsqrt(jnp.mean(xf * xf, axis=-1, keepdims=True) + EPS)
        gain = jnp.where(layer == 0, gain_ref[0:1, :].astype(F32), gain_ref[1:2, :].astype(F32))
        h_ref[:] = (xf * inv * gain).astype(BF16)

        w_cps = proj_copies(layer)
        w_cps[0].wait()
        w_cps[1].wait()
        kvT = project(wkvb[:])
        for t in range(4):
            k = rope(kvT[t * HD:(t + 1) * HD].astype(F32)).astype(BF16)
            k_ref[layer, t * HD:(t + 1) * HD, :] = k
            kf = k.astype(F32)
            kv_send[layer, t, 0:LN, :] = jnp.concatenate([kf[:, 0:LN], kf[:, LN:TOK]], axis=0).T.astype(BF16)
            v = kvT[TOK + t * HD:TOK + (t + 1) * HD]
            v_ref[layer, t * HD:(t + 1) * HD, :] = v
            kv_send[layer, t, LN:LN + HD, :] = v[:, 0:LN]
            kv_send[layer, t, LN + HD:TOK, :] = v[:, LN:TOK]

        @pl.when(layer == 0)
        def _():
            pl.semaphore_wait(barrier, 12 - 2 * me.flag)

        def kv_copy(t):
            return remote(kv_send.at[layer, t], kv.at[me.seq], skv.at[layer, t], rkv.at[layer, me.member], me.target(t), me.core)

        def q_copy(t):
            return remote(q_send.at[layer, t], q_all.at[layer, me.member], sq.at[layer, t], rq.at[layer, me.member], me.target(t), me.core)

        for_others(me.t_self, lambda t: kv_copy(t).start())
        for t in range(4):
            @pl.when(me.t_self(t) == 1)
            def _():
                kv[me.seq] = kv_send[layer, t]

        w_cps[2].wait()
        qT = project(wqb[:])
        for g in range(16):
            q_send[layer, g // 4, (g % 4) * HD:(g % 4 + 1) * HD, :] = rope(qT[g * HD:(g + 1) * HD].astype(F32)).astype(BF16)
        for_others(me.t_self, lambda t: q_copy(t).start())
        for t in range(4):
            @pl.when(me.t_self(t) == 1)
            def _():
                q_all[layer, me.member] = q_send[layer, t]

        def place_of(i, crossed):
            steps = me.steps(i, me.source_mem(i))
            return functools.reduce(lambda a, d: a + steps[d], crossed, me.source(i))

        def ag(i, k):
            dim, crossed = SENDS[k]
            block = kv.at[place_of(i, crossed)]
            return remote(block, block, sag.at[layer], rag.at[layer, i, k], me.seq + me.steps(i, me.mem)[dim], me.head)

        def relay(i, crossed):
            block = kv.at[place_of(i, crossed)]
            remote(block, block, sdd.at[layer], rdd.at[layer, i // 2], me.seq, sib).start()

        def arrived(i, k):
            dim, crossed = SENDS[k]
            block = kv.at[place_of(i, crossed + (dim,))]
            remote(block, block, sag.at[layer], rag.at[layer, i, k], me.seq, sib).wait_recv()
            relay(i, crossed + (dim,))

        def step_own(group):
            for i in group:
                @pl.when(me.s_self(i) == 0)
                def _():
                    remote(kv_send.at[layer, 0], kv.at[me.source(i)], skv.at[layer, 0], rkv.at[layer, i], me.seq, sib).wait_recv()
            for k in (0, 1, 3):
                for i in group:
                    ag(i, k).start()
            for i in group:
                relay(i, ())

        def step_on(group, k, nexts):
            for i in group:
                arrived(i, k)
                for nxt in nexts:
                    ag(i, nxt).start()

        def step_end(group):
            for k in range(3, 7):
                step_on(group, k, ())

        def from_sibling(group):
            half = kv.at[pl.ds(0, 16)]
            remote(half, half, sdd.at[layer], rdd.at[layer, group[0] // 2], me.seq, sib).wait_recv()

        events = (
            (4, step_own, (LOW,)), (7, step_on, (LOW, 0, (2, 4))), (8, step_on, (LOW, 1, (5,))), (10, step_on, (LOW, 2, (6,))),
            (10, step_own, (HIGH,)), (13, step_end, (LOW,)), (14, step_on, (HIGH, 0, (2, 4))))

        def gate_up(n):
            g = jnp.dot(h_ref[:], wgb[n % 3], preferred_element_type=F32)
            u = jnp.dot(h_ref[:], wub[n % 3], preferred_element_type=F32)
            return (g * jax.nn.sigmoid(g) * u).astype(BF16)

        def add_down(hidden, n):
            d = jnp.dot(hidden, wdb[n % 3], preferred_element_type=F32)
            for c in range(8):
                mlp[layer, c] += d[:, c * TOK:(c + 1) * TOK]

        for c in range(8):
            mlp[layer, c] = jnp.zeros((TOK, TOK), F32)
        for c in gu_copies(layer, 0):
            c.wait()
        hid[:] = gate_up(0)
        for c in gu_copies(layer, 3):
            c.start()
        d_copy(layer, 2).start()

        def tile(n, carry):
            for c in gu_copies(layer, n):
                c.wait()
            d_copy(layer, n - 1).wait()
            for at, fn, fn_args in events:
                @pl.when(n == at)
                def _():
                    fn(*fn_args)
            before = hid[:]
            now = gate_up(n)
            add_down(before, n - 1)
            hid[:] = now

            @pl.when(n + 3 < N_TILES)
            def _():
                for c in gu_copies(layer, n + 3):
                    c.start()

            @pl.when(n + 2 < N_TILES)
            def _():
                d_copy(layer, n + 2).start()
            return carry

        lax.fori_loop(1, LAST_BEFORE + 1, tile, 0)
        o_cp = pltpu.make_async_copy(wo.at[layer], wob, osem.at[0])
        o_cp.start()

        @pl.when(layer == 0)
        def _():
            for c in proj_copies(1):
                c.start()
        step_on(HIGH, 1, (5,))
        step_on(HIGH, 2, (6,))
        from_sibling(LOW)
        for_others(me.s_self, lambda i: remote(q_send.at[layer, 0], q_all.at[layer, i], sq.at[layer, 0], rq.at[layer, i], me.seq, sib).wait_recv())

        def o_copy(i):
            return remote(o_send.at[layer, i], o_full.at[layer, me.kv_local], so.at[layer, i], ro.at[layer, me.kv_local], me.source(i), me.mem[2])

        def query(n, carry):
            i = 2 * (n // 2) + (1 - n % 2) * me.head + (n % 2) * (1 - me.head)

            @pl.when(n == 2)
            def _():
                from_sibling(HIGH)

            def store(val):
                o_send[layer, i] = val
            attn_block(me.source(i), q_all[layer, i], kv, store, qa, qb, m_ref, l_ref, acc_ref, sbuf, mx_ref)

            @pl.when(n == 0)
            def _():
                step_end(HIGH)

            @pl.when(me.s_self(i) == 0)
            def _():
                o_copy(i).start()

            @pl.when(me.s_self(i) == 1)
            def _():
                o_full[layer, me.kv_local] = o_send[layer, i]
            return carry

        lax.fori_loop(0, 4, query, 0)
        lax.fori_loop(LAST_BEFORE + 1, N_TILES, tile, 0)
        d_copy(layer, N_TILES - 1).wait()
        add_down(hid[:], N_TILES - 1)

        @pl.when(layer == 0)
        def _():
            first_tiles(1)

        o_cp.wait()
        for_others(me.t_self, lambda t: remote(o_send.at[layer, 0], o_full.at[layer, t], so.at[layer, 0], ro.at[layer, t], me.seq, sib).wait_recv())

        def p_copy(n):
            return remote(mlp.at[layer, n], part_in.at[layer, n], sp.at[layer], rp.at[layer, n], me.seq, sib)

        heads = jnp.concatenate([o_full[layer, t] for t in range(4)], axis=1)
        for n in range(0, 8, 2):
            d = jnp.dot(heads, wob[:, n * TOK:(n + 2) * TOK], preferred_element_type=F32)
            for e in range(2):
                mlp[layer, n + e] += d[:, e * TOK:(e + 1) * TOK]
                p_copy(n + e).start()
        for n in range(8):
            cols = pl.ds(n * TOK, TOK)
            p_copy(n).wait_recv()
            y = (mlp[layer, n] + part_in[layer, n]).astype(BF16)
            x_ref[:, cols] = (x_ref[:, cols].astype(F32) + y.astype(F32)).astype(BF16)
        return carry

    lax.fori_loop(0, 2, layer_body, 0)

    def drain(layer, carry):
        def gone(src, sem):
            remote(src, src, sem, rp.at[layer, 0], me.seq, sib).wait_send()

        for_others(me.t_self, lambda t: gone(kv_send.at[layer, t], skv.at[layer, t]))
        for_others(me.t_self, lambda t: gone(q_send.at[layer, t], sq.at[layer, t]))
        for_others(me.s_self, lambda i: gone(o_send.at[layer, i], so.at[layer, i]))
        gone(kv_all.at[layer, pl.ds(0, 28)], sag.at[layer])
        gone(kv_all.at[layer, pl.ds(0, 32)], sdd.at[layer])
        gone(mlp.at[layer], sp.at[layer])
        return carry

    lax.fori_loop(0, 2, drain, 0)


def vmem(*shape, dtype=BF16):
    return pltpu.VMEM(shape, dtype)


SCRATCH = [
    vmem(32, TOK, dtype=F32), vmem(32, TOK, dtype=F32), vmem(TOK, DM), vmem(2, 4, TOK, TOK), vmem(2, 4, TOK, LN), vmem(2, 4, TOK, TOK), vmem(2, HD, TOK, LN),
    vmem(2, 4, TOK, TOK), vmem(2, 4, TOK, TOK), vmem(2, 8, TOK, TOK, dtype=F32), vmem(2, 8, TOK, TOK, dtype=F32), vmem(TOK, TOK),
    vmem(QW, DM), vmem(2 * TOK, DM), vmem(3, DM, TOK), vmem(3, DM, TOK), vmem(3, TOK, DM), vmem(QW, DM),
    vmem(LN, QW), vmem(LN, QW), vmem(8, QW, dtype=F32), vmem(RC, QW, dtype=F32), vmem(HD, QW, dtype=F32), vmem(2 * TK, QW, dtype=F32), vmem(2 * RC, QW, dtype=F32),
] + [pltpu.SemaphoreType.DMA(s) for s in ((3,), (3,), (3, 3), (1,), (2, 4), (2, 4), (2,), (2,), (2, 4), (2,), (2, 4), (2, 4), (2, 4, 7), (2, 2), (2, 4), (2, 8))]


def solution(mesh):
    row_spec = P(('batch', 'seq'), None)
    pos_spec = P(('batch', 'seq'))
    head_spec = P(None, None, 'head', None)
    out_proj_spec = P(None, 'head', None, None)
    col_spec = P(None, None, 'head')
    down_spec = P(None, 'head', None)
    cache_spec = P(None, ('batch', 'seq'), 'head', None)
    in_vmem = pl.BlockSpec(memory_space=pltpu.VMEM)
    anywhere = pl.BlockSpec(memory_space=pl.ANY)

    def local_forward(x, pos, w_q, w_k, w_v, w_o, w_gate, w_up, w_down, gain):
        cosT, sinT = rope_tables(pos, HD)
        wq = w_q.transpose(0, 2, 3, 1).reshape(2, QW, DM)
        wk = w_k.transpose(0, 2, 3, 1).reshape(2, TOK, DM)
        wv = w_v.transpose(0, 2, 3, 1).reshape(2, TOK, DM)
        wo = w_o.reshape(2, QW, DM)
        x, kT, vT = pl.pallas_call(
            stack_kernel,
            out_shape=OUT_SHAPES,
            in_specs=[anywhere, in_vmem] + [anywhere] * 9,
            out_specs=(in_vmem,) * 3,
            scratch_shapes=SCRATCH,
            compiler_params=pltpu.CompilerParams(collective_id=0, has_side_effects=True, vmem_limit_bytes=VMEM_LIMIT),
            name='stack',
        )(x, gain, cosT, sinT, wq, wk, wv, w_gate, w_up, w_down, wo)
        k_cache = kT.reshape(2, 4, HD, TOK).transpose(0, 3, 1, 2)
        v_cache = vT.reshape(2, 4, HD, TOK).transpose(0, 3, 1, 2)
        return x, k_cache, v_cache

    return jax.shard_map(local_forward, mesh=mesh, in_specs=(row_spec, pos_spec, head_spec, head_spec, head_spec, out_proj_spec, col_spec, col_spec, down_spec, P(None, None)), out_specs=(row_spec, cache_spec, cache_spec), check_vma=False)


OUT_SHAPES = tuple(jax.ShapeDtypeStruct(s, BF16) for s in ((TOK, DM), (2, TOK, TOK), (2, TOK, TOK)))
```

time: 1900 us -> 168 us (0.09)
  starting transfers between devices: 1220 us -> 0 us
  matrix products: 328 us -> 0 us
  Pallas kernels: 0 us -> 159 us
  other arithmetic: 136 us -> 1.52 us
  blocking collectives: 90.6 us -> 0 us
  local copies, waits for them, and re-layouts: 56.6 us -> 5.64 us
  waiting for transfers between devices: 45.9 us -> 0 us
    ppermute x252 -> x0, starting transfers between devices: 1220 us -> none  [the longest x126 879 us: pass_step(): v_blk = lax.ppermute(v_blk, 'seq', shift_pairs)]
    dot_general x268 -> x0, matrix products: 328 us -> none  [the longest x128 152 us: block_update(): jnp.einsum('qkgs,skd->qkgd', prob_f32.astype(jnp.bfloat16), v_blk, prefer...]
    pallas_call x0 -> x1, Pallas kernels: none -> 159 us  [local_forward(): pl.pallas_call(stack_kernel, out_shape=OUT_SHAPES, in_specs=[anywhere, in...]
    reduce_sum x130 -> x0, other arithmetic: 115 us -> none  [the longest x128 113 us: block_update(): row_sum = row_sum * rescale + jnp.sum(prob_f32, axis=-1)]
    psum x2 -> x0, blocking collectives: 90.6 us -> none  [local_forward(): update = lax.psum(part_sum, 'head').astype(jnp.bfloat16)]
    ppermute x252 -> x0, waiting for transfers between devices: 45.9 us -> none  [the longest x126 30.2 us: pass_step(): v_blk = lax.ppermute(v_blk, 'seq', shift_pairs)]
    while x378 -> x0, local copies, waits for them, and re-layouts: 43.7 us -> none
  transfers between devices with their start and end apart: 252 -> 0, of which waited for: 70 -> 0; matrix products, arithmetic and copies ran while one was open for 14% -> 0% of each run, Pallas kernels for 0% -> 0%
where the time goes in v3:
time: 168 us; the launch traced here: 167 us
  Pallas kernels  159 us (95%)
  local copies, waits for them, and re-layouts  5.64 us (3%)
    pallas_call x1, Pallas kernels, local_forward(): pl.pallas_call(stack_kernel, out_shape=OUT_SHAPES, in_specs=[anywhere, in...  159 us
    unnamed x3, local copies, waits for them, and re-layouts  5.64 us

profile of v3, /device:TPU:121, one launch (start us, length us, event | category | flops | bytes accessed | tf_op | source)
XLA Modules:
  0.0 167.2 jit_solution(16074301839907401545)
XLA Ops:
  0.6 0.7 convert_element_type.3
  1.3 0.8 multiply_sine_fusion
  2.2 159.4 %stack.1 = (bf16[256,2048]{1,0:T(8,128)(2,1)}, bf16[2,256,256]{2,1,0:T(8,128)(2,1)}, bf16[2,256,256]{2,1,0:T(8,128)(2,1)}) custom-call(bf16[256,2048]{1,0:T(8,128)(2,1)} %x_hbm.1, bf16[2,2048]{1,0:T(2,128)(2,1)} %gain_ref.1, f32[32,256]{1,0:T(8,128)} %get-tuple-element.10.cos_hbm, f32[32,256]{1,0:T(8,128)} %get-tuple-element.9.sin_hbm, ...), custom_call_target="tpu_custom_call" | custom-call | tf_op jit(solution)/shard_map/stack/pallas_call | solution.py:490
  161.5 2.3 %copy.16 = bf16[256,2048]{1,0:T(8,128)(2,1)} copy(bf16[256,2048]{1,0:T(8,128)(2,1)} %get-tuple-element.14) | data formatting | bytes 2097152
  163.8 1.7 copy.17
  165.5 1.7 copy.18
  (1 shorter events, 0.0 us)

commit v4 on v3

v4 whole, which is shorter than its diff:
```python
import functools
import jax
import jax.numpy as jnp
from jax import lax
from jax.experimental import pallas as pl
from jax.experimental.pallas import tpu as pltpu
from jax.sharding import PartitionSpec as P

ROPE_BASE = 500000.0
EPS = 1e-5
LOG2E = 1.4426950408889634
NEG = -1e30
MESH = pl.DeviceIdType.MESH
TOK, DM, QW, LN, HD = 256, 2048, 1024, 128, 64
F32 = jnp.float32
BF16 = jnp.bfloat16
VMEM_LIMIT = 62 * 1024 * 1024

STRIDE = (1, 4, 16)
N_TILES = 16
NB = 4
TK = NB * TOK
HALF = NB * LN
RC = 8
NT = (((1,), (1,)), ((), ()))
PARTS = ((0,), (1,), (2, 3))
SENDS = ((0, ()), (1, ()), (1, (0,)), (2, ()), (2, (0,)), (2, (1,)), (2, (0, 1)))
SECOND, THIRD = (1, 2), (3, 4, 5, 6)
NEXT = ((2, 4), (5,), (6,), (), (), (), ())
FOUR = range(4)


def rope_tables(positions, head_dim):
    half_dim = head_dim // 2
    inv_freq = ROPE_BASE ** (-(jnp.arange(half_dim, dtype=F32) * 2.0 / head_dim))
    angles = positions.astype(F32)[None, :] * inv_freq[:, None]
    return jnp.cos(angles), jnp.sin(angles)


class Place:
    def __init__(self):
        self.seq = lax.axis_index('seq')
        self.head = lax.axis_index('head')
        self.xyz = (self.seq % 4, (self.seq // 4) % 4, self.seq // 16)
        self.mem = tuple(c // 2 for c in self.xyz)
        self.cls = tuple(((c + 1) // 2) % 2 for c in self.xyz)
        self.core = (self.mem[0] + self.mem[1]) % 2
        self.kv_local = 2 * self.mem[1] + self.mem[0]
        self.member = 2 * self.mem[2] + self.mem[1]
        same_z = 1 - lax.rem(self.head + self.mem[2], 2)
        self.flag = same_z * (1 - lax.rem(self.head + self.core, 2))

    def at(self, mem):
        cs = [m * 3 + c * (1 - 2 * m) for m, c in zip(mem, self.cls)]
        return cs[2] * 16 + cs[1] * 4 + cs[0]

    def target(self, t):
        return self.at((t % 2, t // 2, self.head))

    def source_mem(self, i):
        my = i % 2
        return ((my + self.head) % 2, my, i // 2)

    def source(self, i):
        return self.at(self.source_mem(i))

    def steps(self, i, mem):
        d = [(1 - 2 * c) * (1 - 2 * m) * s for c, m, s in zip(self.cls, mem, STRIDE)]
        turns = [d[k:] + d[:k] for k in range(3)]
        first, other = ((0, 1), (2, 0), (1, 1), (2, 2))[i]
        return [a * (1 - self.head) + b * self.head for a, b in zip(turns[first], turns[other])]

    def across(self, i, crossed):
        steps = self.steps(i, self.source_mem(i))
        return functools.reduce(lambda a, d: a + steps[d], crossed, self.source(i))

    def second(self, t):
        mem = (t % 2, t // 2, self.head)
        d = [(1 - 2 * c) * (1 - 2 * m) * s for c, m, s in zip(self.cls, mem, STRIDE)]
        low = d[0] * (1 - self.core) + d[1] * self.core
        high = d[2] * (1 - self.core) + d[0] * self.core
        return self.at(mem) + low * (1 - self.mem[1]) + high * self.mem[1]

    def s_self(self, i):
        return self.flag * (1 - lax.rem(i // 2 + self.mem[2], 2)) * (1 - lax.rem(i % 2 + self.mem[1], 2))

    def t_self(self, t):
        return self.flag * (1 - lax.rem(t // 2 + self.mem[1], 2)) * (1 - lax.rem(t % 2 + self.mem[0], 2))


def fold_max(x):
    return jnp.max(x.reshape(x.shape[0] // RC, RC, x.shape[1]), axis=0)


def fold_sum(x):
    return jnp.sum(x.reshape(x.shape[0] // RC, RC, x.shape[1]), axis=0)


def attn_logits(first, c, kv_all, qa, qb, sbuf, off, mx_ref, moff):
    cols = pl.ds(c * TOK, TOK)
    keys = kv_all[pl.ds(first, NB), 0:LN, :].reshape(HALF, LN)
    sa = jnp.dot(keys, qa[:, cols], preferred_element_type=F32) * (LOG2E / 8.0)
    sb = jnp.dot(keys, qb[:, cols], preferred_element_type=F32) * (LOG2E / 8.0)
    sbuf[pl.ds(off, HALF), cols] = sa
    sbuf[pl.ds(off + HALF, HALF), cols] = sb
    mx_ref[pl.ds(moff, RC), cols] = jnp.maximum(fold_max(sa), fold_max(sb))


def attn_update(cols, mx, parts, vTs, m_ref, l_ref, acc_ref):
    m_old = m_ref[0:1, cols]
    m_new = jnp.maximum(m_old, jnp.max(mx, axis=0, keepdims=True))
    alpha = jnp.exp2(m_old - m_new)
    m_ref[:, cols] = jnp.broadcast_to(m_new, (8, TOK))
    lsum = l_ref[:, cols] * alpha
    ps = []
    for s in parts:
        p = jnp.exp2(s - m_new)
        lsum = lsum + fold_sum(p)
        ps.append(p.astype(BF16))
    l_ref[:, cols] = lsum
    pv = jnp.dot(jnp.concatenate(vTs, axis=1), jnp.concatenate(ps, axis=0), preferred_element_type=F32)
    acc_ref[:, cols] = acc_ref[:, cols] * alpha + pv


def values_of(kv_all, first, blocks):
    return [kv_all[first + b, LN + HD * h:192 + HD * h, :] for h in range(2) for b in range(blocks)]


def attn_tail(first, t, kv_all, sbuf, off, m_ref, l_ref, acc_ref):
    for c in FOUR:
        cols = pl.ds(c * TOK, TOK)
        ti = lax.broadcasted_iota(jnp.int32, (LN, TOK), 1)
        ki = lax.broadcasted_iota(jnp.int32, (LN, TOK), 0)
        parts = []
        for h in range(2):
            base = pl.multiple_of(off + h * HALF, LN)
            if t > 0:
                parts.append(sbuf[pl.ds(base, t * LN), cols])
            parts.append(jnp.where(ki + h * LN <= ti, sbuf[pl.ds(base + t * LN, LN), cols], NEG))
        mx = functools.reduce(jnp.maximum, [fold_max(p) for p in parts])
        attn_update(cols, mx, parts, values_of(kv_all, first, t + 1), m_ref, l_ref, acc_ref)


def attn_start(i, qT, state):
    qa, qb, m_ref, l_ref, acc_ref, _, _ = state
    zero = jnp.zeros((HD, TOK), BF16)
    for g in FOUR:
        q = qT[g * HD:(g + 1) * HD, :]
        cols = pl.ds(g * TOK, TOK)
        qa[i, :, cols] = jnp.concatenate([q, zero], axis=0)
        qb[i, :, cols] = jnp.concatenate([zero, q], axis=0)
    m_ref[i] = jnp.full((8, QW), NEG, F32)
    l_ref[i] = jnp.zeros((RC, QW), F32)
    acc_ref[i] = jnp.zeros((HD, QW), F32)


def attn_step(now, then, p, kv, state):
    qa, qb, m_ref, l_ref, acc_ref, sbuf, mx_ref = state
    i, group = now
    j, after = then
    for c in FOUR:
        attn_logits(after * NB, c, kv, qa.at[j], qb.at[j], sbuf, (1 - p) * TK, mx_ref, (1 - p) * RC)
        cols = pl.ds(c * TOK, TOK)
        attn_update(cols, mx_ref[pl.ds(p * RC, RC), cols], [sbuf[pl.ds(p * TK, TK), cols]], values_of(kv, group * NB, NB), m_ref.at[i], l_ref.at[i], acc_ref.at[i])


def attn_prime(i, group, kv, state):
    qa, qb, _, _, _, sbuf, mx_ref = state
    for c in FOUR:
        attn_logits(group * NB, c, kv, qa.at[i], qb.at[i], sbuf, 0, mx_ref, 0)


def attn_early(part, kv, state):
    def at(s):
        last = s // 8
        more = 1 - last * part
        return (2 + s // 4 - last) * more, ((s % 4) // 2 * 4 + 2 * part + s % 2) * more

    attn_prime(2, 2 * part, kv, state)

    def turn(n, carry):
        for e in FOUR:
            attn_step(at(4 * n + e), at(4 * n + e + 1), e % 2, kv, state)
        return carry

    lax.fori_loop(0, 2, turn, 0)


def attn_block(i, pos, kv, state):
    qa, qb, m_ref, l_ref, acc_ref, sbuf, mx_ref = state
    first = i // 2 * 8
    groups = pos // NB - first

    @pl.when(i > 0)
    def _():
        attn_prime(i, first, kv, state)

    def one(n, p):
        attn_step((i, first + n), (i, first + n + 1), p, kv, state)

    done = groups // 4 * 4

    @pl.when(groups >= 4)
    def _():
        for n in FOUR:
            one(n, n % 2)

    @pl.when(groups - done >= 2)
    def _():
        one(done, 0)
        one(done + 1, 1)

    @pl.when(groups % 2 == 1)
    def _():
        one(groups - 1, 0)
    for t in range(NB):
        @pl.when(pos % NB == t)
        def _():
            attn_tail(pos // NB * NB, t, kv, sbuf, (groups % 2) * TK, m_ref.at[i], l_ref.at[i], acc_ref.at[i])
    oT = acc_ref[i] / jnp.sum(l_ref[i], axis=0, keepdims=True)
    halves = []
    for g in range(0, 4, 2):
        two = jnp.concatenate([oT[:, g * TOK:(g + 1) * TOK], oT[:, (g + 1) * TOK:(g + 2) * TOK]], axis=0)
        halves.append(two.T.astype(BF16))
    return jnp.concatenate(halves, axis=1)


def stack_kernel(x_hbm, gain_ref, cos_hbm, sin_hbm, wq, wk, wv, wg, wu, wd, wo, x_ref, k_ref, v_ref,
                 cosT, sinT, h_ref, q_send, kv_send, q_all, kv_all, o_send, o_full, mlp, part_in, hid, wqb, wkvb, wgb, wub, wdb, wob,
                 qa, qb, m_ref, l_ref, acc_ref, sbuf, mx_ref,
                 xsem, wsem, msem, osem, skv, sq, sag, sdd, so, sp, rkv, rq, rag, rdd, ro, rp):
    me = Place()
    sib = 1 - me.head
    state = (qa, qb, m_ref, l_ref, acc_ref, sbuf, mx_ref)

    def remote(src, dst, ssem, rsem, seq, head):
        return pltpu.make_async_remote_copy(src_ref=src, dst_ref=dst, send_sem=ssem, recv_sem=rsem, device_id={'seq': seq, 'head': head}, device_id_type=MESH)

    def for_others(is_self, fn):
        for i in FOUR:
            @pl.when(is_self(i) == 0)
            def _():
                fn(i)

    start_cps = [pltpu.make_async_copy(x_hbm, x_ref, xsem.at[0]), pltpu.make_async_copy(cos_hbm, cosT, xsem.at[1]), pltpu.make_async_copy(sin_hbm, sinT, xsem.at[2])]

    def proj_copies(layer):
        return (pltpu.make_async_copy(wk.at[layer], wkvb.at[pl.ds(0, TOK)], wsem.at[0]), pltpu.make_async_copy(wv.at[layer], wkvb.at[pl.ds(TOK, TOK)], wsem.at[1]), pltpu.make_async_copy(wq.at[layer], wqb, wsem.at[2]))

    for c in start_cps:
        c.start()
    for n in range(2):
        proj_copies(0)[n].start()

    barrier = pltpu.get_barrier_semaphore()

    def hello(seq, head):
        pl.semaphore_signal(barrier, inc=1, device_id={'seq': seq, 'head': head}, device_id_type=MESH)

    for_others(me.s_self, lambda i: hello(me.source(i), me.mem[2]))
    for_others(me.t_self, lambda t: hello(me.target(t), me.core))
    for i in range(2):
        hello(me.across(i, (0,)), me.mem[2])
    for step in me.steps(0, me.mem):
        hello(me.seq + step, me.head)
    hello(me.seq, sib)

    def gu_copies(layer, n):
        off = pl.multiple_of(n * TOK, TOK)
        slot = n % 3
        return (pltpu.make_async_copy(wg.at[layer, :, pl.ds(off, TOK)], wgb.at[slot], msem.at[0, slot]), pltpu.make_async_copy(wu.at[layer, :, pl.ds(off, TOK)], wub.at[slot], msem.at[1, slot]))

    def d_copy(layer, n):
        return pltpu.make_async_copy(wd.at[layer, pl.ds(pl.multiple_of(n * TOK, TOK), TOK)], wdb.at[n % 3], msem.at[2, n % 3])

    def first_tiles(layer):
        for n in range(3):
            for c in gu_copies(layer, n):
                c.start()
        for n in range(2):
            d_copy(layer, n).start()

    for c in start_cps:
        c.wait()
    proj_copies(0)[2].start()

    def rope(a):
        lo, hi = a[0:32], a[32:HD]
        return jnp.concatenate([lo * cosT[:] - hi * sinT[:], hi * cosT[:] + lo * sinT[:]], axis=0)

    def project(w):
        return lax.dot_general(w, h_ref[:], NT, preferred_element_type=F32).astype(BF16)

    def layer_body(layer, carry):
        kv = kv_all.at[layer]
        xf = x_ref[:].astype(F32)
        inv = lax.rsqrt(jnp.mean(xf * xf, axis=-1, keepdims=True) + EPS)
        gain = jnp.where(layer == 0, gain_ref[0:1, :].astype(F32), gain_ref[1:2, :].astype(F32))
        h_ref[:] = (xf * inv * gain).astype(BF16)

        w_cps = proj_copies(layer)
        w_cps[0].wait()
        w_cps[1].wait()
        kvT = project(wkvb[:])
        for t in FOUR:
            k = rope(kvT[t * HD:(t + 1) * HD].astype(F32)).astype(BF16)
            k_ref[layer, t * HD:(t + 1) * HD, :] = k
            kf = k.astype(F32)
            kv_send[layer, t, 0:LN, :] = jnp.concatenate([kf[:, :LN], kf[:, LN:TOK]], axis=0).T.astype(BF16)
            v = kvT[TOK + t * HD:TOK + (t + 1) * HD]
            v_ref[layer, t * HD:(t + 1) * HD, :] = v
            kv_send[layer, t, LN:LN + HD, :] = v[:, :LN]
            kv_send[layer, t, LN + HD:TOK, :] = v[:, LN:TOK]

        @pl.when(layer == 0)
        def _():
            first_tiles(0)

        @pl.when(layer == 0)
        def _():
            pl.semaphore_wait(barrier, 12 - 2 * me.flag + 4 * (1 - me.mem[2]))

        def kv_copy(t):
            return remote(kv_send.at[layer, t], kv.at[me.seq], skv.at[layer, t], rkv.at[layer, me.member], me.target(t), me.core)

        def q_copy(t):
            return remote(q_send.at[layer, t], q_all.at[layer, me.member], sq.at[layer, t], rq.at[layer, me.member], me.target(t), me.core)

        def second_copy(t):
            return remote(kv_send.at[layer, t], kv.at[me.seq], skv.at[layer, 4 + t], rag.at[layer, me.mem[1], 0], me.second(t), me.core)

        for_others(me.t_self, lambda t: kv_copy(t).start())

        @pl.when(me.mem[2] == 0)
        def _():
            for t in FOUR:
                second_copy(t).start()
        for t in FOUR:
            @pl.when(me.t_self(t) == 1)
            def _():
                kv[me.seq] = kv_send[layer, t]

        w_cps[2].wait()
        for t in FOUR:
            qT = project(wqb[t * TOK:(t + 1) * TOK])
            for g in FOUR:
                q_send[layer, t, g * HD:(g + 1) * HD, :] = rope(qT[g * HD:(g + 1) * HD].astype(F32)).astype(BF16)

        def send_queries():
            for_others(me.t_self, lambda t: q_copy(t).start())
            for t in FOUR:
                @pl.when(me.t_self(t) == 1)
                def _():
                    q_all[layer, me.member] = q_send[layer, t]

        def ag(i, k):
            dim, crossed = SENDS[k]
            block = kv.at[me.across(i, crossed)]
            return remote(block, block, sag.at[layer], rag.at[layer, i, k], me.seq + me.steps(i, me.mem)[dim], me.head)

        def relay(i, crossed):
            block = kv.at[me.across(i, crossed)]
            remote(block, block, sdd.at[layer], rdd.at[layer, min(i, 2)], me.seq, sib).start()

        def arrived(i, k):
            dim, crossed = SENDS[k]
            block = kv.at[me.across(i, crossed + (dim,))]
            remote(block, block, sag.at[layer], rag.at[layer, i, k], me.seq, sib).wait_recv()

        def step(part, number):
            members = PARTS[part]
            if number == 0:
                for i in members:
                    @pl.when(me.s_self(i) == 0)
                    def _():
                        remote(kv_send.at[layer, 0], kv.at[me.source(i)], skv.at[layer, 0], rkv.at[layer, i], me.seq, sib).wait_recv()
                for k in ((1, 3) if part < 2 else (0, 1, 3)):
                    for i in members:
                        ag(i, k).start()
                for i in members:
                    relay(i, ())
            first = (0,) if number == (part == 2) else ()
            waits = first if number < 2 else SECOND if number == 2 else THIRD
            for k in waits:
                for i in members:
                    arrived(i, k)
                    for nxt in NEXT[k]:
                        ag(i, nxt).start()
            for k in waits:
                for i in members:
                    relay(i, SENDS[k][1] + (SENDS[k][0],))

        def from_sibling(part):
            blocks = kv.at[pl.ds(0, 8 * len(PARTS[part]))]
            remote(blocks, blocks, sdd.at[layer], rdd.at[layer, part], me.seq, sib).wait_recv()

        def gate_up(n):
            g = jnp.dot(h_ref[:], wgb[n % 3], preferred_element_type=F32)
            u = jnp.dot(h_ref[:], wub[n % 3], preferred_element_type=F32)
            return (g * jax.nn.sigmoid(g) * u).astype(BF16)

        def add_down(hidden, n):
            d = jnp.dot(hidden, wdb[n % 3], preferred_element_type=F32)
            for c in range(8):
                part = d[:, c * TOK:(c + 1) * TOK]
                mlp[layer, c] = part if n == 0 else mlp[layer, c] + part

        for c in gu_copies(layer, 0):
            c.wait()
        hid[:] = gate_up(0)
        for c in gu_copies(layer, 3):
            c.start()
        d_copy(layer, 2).start()

        def tile(n):
            for c in gu_copies(layer, n):
                c.wait()
            d_copy(layer, n - 1).wait()
            before = hid[:]
            now = gate_up(n)
            add_down(before, n - 1)
            hid[:] = now
            if n + 3 < N_TILES:
                for c in gu_copies(layer, n + 3):
                    c.start()
            if n + 2 < N_TILES:
                d_copy(layer, n + 2).start()

        for n in range(1, BEFORE):
            for part, number in EVENTS.get(n, ()):
                step(part, number)
            if n == 7:
                send_queries()
            tile(n)

        o_cp = pltpu.make_async_copy(wo.at[layer], wob, osem.at[0])
        o_cp.start()

        @pl.when(layer == 0)
        def _():
            for c in proj_copies(1):
                c.start()
        for part, number in EVENTS[BEFORE]:
            step(part, number)
        for_others(me.s_self, lambda i: remote(q_send.at[layer, 0], q_all.at[layer, i], sq.at[layer, 0], rq.at[layer, i], me.seq, sib).wait_recv())
        from_sibling(0)

        def o_copy(i):
            return remote(o_send.at[layer, i], o_full.at[layer, me.kv_local], so.at[layer, i], ro.at[layer, me.kv_local], me.source(i), me.mem[2])

        lax.fori_loop(0, 4, lambda i, carry: attn_start(i, q_all[layer, i], state) or carry, 0)
        def early(part, carry):
            attn_early(part, kv, state)
            @pl.when(part == 0)
            def _():
                for which, number in EVENTS[N_TILES]:
                    step(which, number)
                from_sibling(1)

            @pl.when(part == 1)
            def _():
                for which, number in EVENTS[N_TILES + 1]:
                    step(which, number)
            return carry

        lax.fori_loop(0, 2, early, 0)

        def query(i, carry):
            @pl.when(i == 2)
            def _():
                from_sibling(2)

            o_send[layer, i] = attn_block(i, me.source(i), kv, state)

            @pl.when(me.s_self(i) == 0)
            def _():
                o_copy(i).start()

            @pl.when(me.s_self(i) == 1)
            def _():
                o_full[layer, me.kv_local] = o_send[layer, i]
            return carry

        lax.fori_loop(0, 4, query, 0)
        for n in range(BEFORE, N_TILES):
            tile(n)
        d_copy(layer, N_TILES - 1).wait()
        add_down(hid[:], N_TILES - 1)

        @pl.when(layer == 0)
        def _():
            first_tiles(1)

        o_cp.wait()
        for_others(me.t_self, lambda t: remote(o_send.at[layer, 0], o_full.at[layer, t], so.at[layer, 0], ro.at[layer, t], me.seq, sib).wait_recv())

        def p_copy(n):
            return remote(mlp.at[layer, n], part_in.at[layer, n], sp.at[layer], rp.at[layer, n], me.seq, sib)

        heads = jnp.concatenate([o_full[layer, t] for t in FOUR], axis=1)
        for n in range(0, 8, 2):
            d = jnp.dot(heads, wob[:, n * TOK:(n + 2) * TOK], preferred_element_type=F32)
            for e in range(2):
                mlp[layer, n + e] += d[:, e * TOK:(e + 1) * TOK]
                p_copy(n + e).start()
        for n in range(8):
            cols = pl.ds(n * TOK, TOK)
            p_copy(n).wait_recv()
            y = (mlp[layer, n] + part_in[layer, n]).astype(BF16)
            x_ref[:, cols] = (x_ref[:, cols].astype(F32) + y.astype(F32)).astype(BF16)
        return carry

    lax.fori_loop(0, 2, layer_body, 0)

    def drain(layer, carry):
        def gone(src, sem):
            remote(src, src, sem, rp.at[layer, 0], me.seq, sib).wait_send()

        for_others(me.t_self, lambda t: gone(kv_send.at[layer, t], skv.at[layer, t]))
        for_others(me.t_self, lambda t: gone(q_send.at[layer, t], sq.at[layer, t]))
        for_others(me.s_self, lambda i: gone(o_send.at[layer, i], so.at[layer, i]))
        gone(kv_all.at[layer, pl.ds(0, 26)], sag.at[layer])

        @pl.when(me.mem[2] == 0)
        def _():
            for t in FOUR:
                gone(kv_send.at[layer, t], skv.at[layer, 4 + t])
        gone(kv_all.at[layer, pl.ds(0, 32)], sdd.at[layer])
        gone(mlp.at[layer], sp.at[layer])
        return carry

    lax.fori_loop(0, 2, drain, 0)


def finish_kernel(x_in, k_in, v_in, x_out, k_out, v_out, sem):
    cps = [pltpu.make_async_copy(a, b, sem.at[n]) for n, (a, b) in enumerate(((x_in, x_out), (k_in, k_out), (v_in, v_out)))]
    for c in cps:
        c.start()
    for c in cps:
        c.wait()


def vmem(*shape, dtype=BF16):
    return pltpu.VMEM(shape, dtype)


BEFORE = 15
EVENTS = {5: ((0, 0),), 6: ((1, 0),), 9: ((0, 2),), 10: ((1, 2),), 12: ((2, 0),), 13: ((0, 4),), 15: ((1, 4), (2, 1)), 16: ((2, 2),), 17: ((2, 4),)}


SCRATCH = [
    vmem(32, TOK, dtype=F32), vmem(32, TOK, dtype=F32), vmem(TOK, DM), vmem(2, 4, TOK, TOK), vmem(2, 4, TOK, LN), vmem(2, 4, TOK, TOK), vmem(2, HD, TOK, LN),
    vmem(2, 4, TOK, TOK), vmem(2, 4, TOK, TOK), vmem(2, 8, TOK, TOK, dtype=F32), vmem(2, 8, TOK, TOK, dtype=F32), vmem(TOK, TOK),
    vmem(QW, DM), vmem(2 * TOK, DM), vmem(3, DM, TOK), vmem(3, DM, TOK), vmem(3, TOK, DM), vmem(QW, DM),
    vmem(4, LN, QW), vmem(4, LN, QW), vmem(4, 8, QW, dtype=F32), vmem(4, RC, QW, dtype=F32), vmem(4, HD, QW, dtype=F32), vmem(2 * TK, QW, dtype=F32), vmem(2 * RC, QW, dtype=F32),
] + [pltpu.SemaphoreType.DMA(s) for s in ((3,), (3,), (3, 3), (1,), (2, 8), (2, 4), (2,), (2,), (2, 4), (2,), (2, 4), (2, 4), (2, 4, 7), (2, 3), (2, 4), (2, 8))]


def solution(mesh):
    row_spec = P(('batch', 'seq'), None)
    pos_spec = P(('batch', 'seq'))
    head_spec = P(None, None, 'head', None)
    out_proj_spec = P(None, 'head', None, None)
    col_spec = P(None, None, 'head')
    down_spec = P(None, 'head', None)
    cache_spec = P(None, ('batch', 'seq'), 'head', None)
    in_vmem = pl.BlockSpec(memory_space=pltpu.VMEM)
    anywhere = pl.BlockSpec(memory_space=pl.ANY)

    def local_forward(x, pos, w_q, w_k, w_v, w_o, w_gate, w_up, w_down, gain):
        cosT, sinT = rope_tables(pos, HD)
        wq = w_q.transpose(0, 2, 3, 1).reshape(2, QW, DM)
        wk = w_k.transpose(0, 2, 3, 1).reshape(2, TOK, DM)
        wv = w_v.transpose(0, 2, 3, 1).reshape(2, TOK, DM)
        wo = w_o.reshape(2, QW, DM)
        x, kT, vT = pl.pallas_call(
            stack_kernel,
            out_shape=tuple(pltpu.VMEM(s, BF16) for s in OUT_SHAPES),
            in_specs=[anywhere, in_vmem] + [anywhere] * 9,
            out_specs=(in_vmem,) * 3,
            scratch_shapes=SCRATCH,
            compiler_params=pltpu.CompilerParams(collective_id=0, has_side_effects=True, vmem_limit_bytes=VMEM_LIMIT),
            name='stack',
        )(x, gain, cosT, sinT, wq, wk, wv, w_gate, w_up, w_down, wo)
        x, kT, vT = pl.pallas_call(
            finish_kernel,
            out_shape=tuple(jax.ShapeDtypeStruct(s, BF16) for s in OUT_SHAPES),
            in_specs=[in_vmem] * 3,
            out_specs=(anywhere,) * 3,
            scratch_shapes=[pltpu.SemaphoreType.DMA((3,))],
            compiler_params=pltpu.CompilerParams(vmem_limit_bytes=QW * QW),
            name='finish',
        )(*[pltpu.with_memory_space_constraint(a, pltpu.VMEM) for a in (x, kT, vT)])
        k_cache = kT.reshape(2, 4, HD, TOK).transpose(0, 3, 1, 2)
        v_cache = vT.reshape(2, 4, HD, TOK).transpose(0, 3, 1, 2)
        return x, k_cache, v_cache

    return jax.shard_map(local_forward, mesh=mesh, in_specs=(row_spec, pos_spec, head_spec, head_spec, head_spec, out_proj_spec, col_spec, col_spec, down_spec, P(None, None)), out_specs=(row_spec, cache_spec, cache_spec), check_vma=False)


OUT_SHAPES = ((TOK, DM), (2, TOK, TOK), (2, TOK, TOK))
```

time: 168 us -> 144 us (0.86)
  Pallas kernels: 159 us -> 142 us
  local copies, waits for them, and re-layouts: 5.64 us -> 0 us
    pallas_call x1 -> x2, Pallas kernels: 159 us -> 142 us  [the longest x1 141 us: local_forward(): pl.pallas_call(stack_kernel, out_shape=tuple((pltpu.VMEM(s, BF16) for s i...]
    unnamed x3 -> x0, local copies, waits for them, and re-layouts: 5.64 us -> none
where the time goes in v4:
time: 144 us
  Pallas kernels  142 us (99%)
  other arithmetic  1.52 us (1%)
    pallas_call x1, Pallas kernels, local_forward(): pl.pallas_call(stack_kernel, out_shape=tuple((pltpu.VMEM(s, BF16) for s i...  141 us

profile of v4, /device:TPU:121, one launch (start us, length us, event | category | flops | bytes accessed | tf_op | source)
XLA Modules:
  0.0 144.0 jit_solution(10388279589103242457)
XLA Ops:
  0.6 0.7 convert_element_type.3
  1.3 0.8 multiply_sine_fusion
  2.2 140.7 %stack.1 = (bf16[256,2048]{1,0:T(8,128)(2,1)S(1)}, bf16[2,256,256]{2,1,0:T(8,128)(2,1)S(1)}, bf16[2,256,256]{2,1,0:T(8,128)(2,1)S(1)}) custom-call(bf16[256,2048]{1,0:T(8,128)(2,1)} %x_hbm.1, bf16[2,2048]{1,0:T(2,128)(2,1)} %gain_ref.1, f32[32,256]{1,0:T(8,128)} %get-tuple-element.16.cos_hbm, f32[32,256]{1,0:T(8,128)} %get-tuple-element.15.sin_hbm, ...), custom_call_target="tpu_custom_call" | custom-call | tf_op jit(solution)/shard_map/stack/pallas_call | solution.py:576
  142.8 1.2 finish.1
  (1 shorter events, 0.0 us)

commit v5 on v4

--- a/solution.py
+++ b/solution.py
@@ -28,13 +28,6 @@
 SECOND, THIRD = (1, 2), (3, 4, 5, 6)
 NEXT = ((2, 4), (5,), (6,), (), (), (), ())
 FOUR = range(4)
-
-
-def rope_tables(positions, head_dim):
-    half_dim = head_dim // 2
-    inv_freq = ROPE_BASE ** (-(jnp.arange(half_dim, dtype=F32) * 2.0 / head_dim))
-    angles = positions.astype(F32)[None, :] * inv_freq[:, None]
-    return jnp.cos(angles), jnp.sin(angles)
 
 
 class Place:
@@ -170,20 +163,18 @@
         attn_logits(group * NB, c, kv, qa.at[i], qb.at[i], sbuf, 0, mx_ref, 0)
 
 
-def attn_early(part, kv, state):
+def attn_early(n, kv, state):
     def at(s):
-        last = s // 8
-        more = 1 - last * part
-        return (2 + s // 4 - last) * more, ((s % 4) // 2 * 4 + 2 * part + s % 2) * more
-
-    attn_prime(2, 2 * part, kv, state)
-
-    def turn(n, carry):
-        for e in FOUR:
-            attn_step(at(4 * n + e), at(4 * n + e + 1), e % 2, kv, state)
-        return carry
-
-    lax.fori_loop(0, 2, turn, 0)
+        s = 4 * n + s
+        more = 1 - s // 16
+        return (2 + s // 4 % 2) * more, ((s % 4) // 2 * 4 + 2 * (s // 8) + s % 2) * more
+
+    @pl.when(n % 2 == 0)
+    def _():
+        attn_prime(2, n, kv, state)
+    for e in FOUR:
+        ahead = at(e + 1) if e < 3 else tuple(jnp.where(n == 1, a, b) for a, b in zip(at(e), at(e + 1)))
+        attn_step(at(e), ahead, e % 2, kv, state)
 
 
 def attn_block(i, pos, kv, state):
@@ -225,7 +216,7 @@
     return jnp.concatenate(halves, axis=1)
 
 
-def stack_kernel(x_hbm, gain_ref, cos_hbm, sin_hbm, wq, wk, wv, wg, wu, wd, wo, x_ref, k_ref, v_ref,
+def stack_kernel(x_hbm, gain_ref, pos_ref, wq, wk, wv, wg, wu, wd, wo, x_ref, k_ref, v_ref,
                  cosT, sinT, h_ref, q_send, kv_send, q_all, kv_all, o_send, o_full, mlp, part_in, hid, wqb, wkvb, wgb, wub, wdb, wob,
                  qa, qb, m_ref, l_ref, acc_ref, sbuf, mx_ref,
                  xsem, wsem, msem, osem, skv, sq, sag, sdd, so, sp, rkv, rq, rag, rdd, ro, rp):
@@ -242,7 +233,7 @@
             def _():
                 fn(i)
 
-    start_cps = [pltpu.make_async_copy(x_hbm, x_ref, xsem.at[0]), pltpu.make_async_copy(cos_hbm, cosT, xsem.at[1]), pltpu.make_async_copy(sin_hbm, sinT, xsem.at[2])]
+    start_cps = [pltpu.make_async_copy(x_hbm, x_ref, xsem.at[0])]
 
     def proj_copies(layer):
         return (pltpu.make_async_copy(wk.at[layer], wkvb.at[pl.ds(0, TOK)], wsem.at[0]), pltpu.make_async_copy(wv.at[layer], wkvb.at[pl.ds(TOK, TOK)], wsem.at[1]), pltpu.make_async_copy(wq.at[layer], wqb, wsem.at[2]))
@@ -280,6 +271,10 @@
         for n in range(2):
             d_copy(layer, n).start()
 
+    freq = ROPE_BASE ** (-(lax.broadcasted_iota(jnp.int32, (HD // 2, TOK), 0).astype(F32) * 2.0 / HD))
+    angles = pos_ref[:].astype(F32) * freq
+    cosT[:] = jnp.cos(angles)
+    sinT[:] = jnp.sin(angles)
     for c in start_cps:
         c.wait()
     proj_copies(0)[2].start()
@@ -301,13 +296,14 @@
         w_cps = proj_copies(layer)
         w_cps[0].wait()
         w_cps[1].wait()
-        kvT = project(wkvb[:])
+        kT = project(wkvb[:TOK])
+        vT = project(wkvb[TOK:])
         for t in FOUR:
-            k = rope(kvT[t * HD:(t + 1) * HD].astype(F32)).astype(BF16)
+            k = rope(kT[t * HD:(t + 1) * HD].astype(F32)).astype(BF16)
             k_ref[layer, t * HD:(t + 1) * HD, :] = k
             kf = k.astype(F32)
             kv_send[layer, t, 0:LN, :] = jnp.concatenate([kf[:, :LN], kf[:, LN:TOK]], axis=0).T.astype(BF16)
-            v = kvT[TOK + t * HD:TOK + (t + 1) * HD]
+            v = vT[t * HD:(t + 1) * HD]
             v_ref[layer, t * HD:(t + 1) * HD, :] = v
             kv_send[layer, t, LN:LN + HD, :] = v[:, :LN]
             kv_send[layer, t, LN + HD:TOK, :] = v[:, LN:TOK]
@@ -429,7 +425,7 @@
         for n in range(1, BEFORE):
             for part, number in EVENTS.get(n, ()):
                 step(part, number)
-            if n == 7:
+            if n == 4:
                 send_queries()
             tile(n)
 
@@ -449,21 +445,18 @@
             return remote(o_send.at[layer, i], o_full.at[layer, me.kv_local], so.at[layer, i], ro.at[layer, me.kv_local], me.source(i), me.mem[2])
 
         lax.fori_loop(0, 4, lambda i, carry: attn_start(i, q_all[layer, i], state) or carry, 0)
-        def early(part, carry):
-            attn_early(part, kv, state)
-            @pl.when(part == 0)
-            def _():
-                for which, number in EVENTS[N_TILES]:
-                    step(which, number)
-                from_sibling(1)
-
-            @pl.when(part == 1)
-            def _():
-                for which, number in EVENTS[N_TILES + 1]:
-                    step(which, number)
+        def early(n, carry):
+            attn_early(n, kv, state)
+            for e in FOUR:
+                @pl.when(n == e)
+                def _():
+                    for which, number in EVENTS[N_TILES + e]:
+                        step(which, number)
+                    if e == 1:
+                        from_sibling(1)
             return carry
 
-        lax.fori_loop(0, 2, early, 0)
+        lax.fori_loop(0, 4, early, 0)
 
         def query(i, carry):
             @pl.when(i == 2)
@@ -471,6 +464,11 @@
                 from_sibling(2)
 
             o_send[layer, i] = attn_block(i, me.source(i), kv, state)
+
+            @pl.when(i == 0)
+            def _():
+                for part, number in EVENTS[N_TILES + 4]:
+                    step(part, number)
 
             @pl.when(me.s_self(i) == 0)
             def _():
@@ -545,7 +543,7 @@
 
 
 BEFORE = 15
-EVENTS = {5: ((0, 0),), 6: ((1, 0),), 9: ((0, 2),), 10: ((1, 2),), 12: ((2, 0),), 13: ((0, 4),), 15: ((1, 4), (2, 1)), 16: ((2, 2),), 17: ((2, 4),)}
+EVENTS = {5: ((0, 0),), 7: ((1, 0),), 9: ((0, 2),), 11: ((1, 2),), 12: ((2, 0),), 13: ((0, 4),), 15: (), 16: ((1, 4), (2, 1)), 17: (), 18: ((2, 2),), 19: (), 20: ((2, 4),)}
 
 
 SCRATCH = [
@@ -553,7 +551,7 @@
     vmem(2, 4, TOK, TOK), vmem(2, 4, TOK, TOK), vmem(2, 8, TOK, TOK, dtype=F32), vmem(2, 8, TOK, TOK, dtype=F32), vmem(TOK, TOK),
     vmem(QW, DM), vmem(2 * TOK, DM), vmem(3, DM, TOK), vmem(3, DM, TOK), vmem(3, TOK, DM), vmem(QW, DM),
     vmem(4, LN, QW), vmem(4, LN, QW), vmem(4, 8, QW, dtype=F32), vmem(4, RC, QW, dtype=F32), vmem(4, HD, QW, dtype=F32), vmem(2 * TK, QW, dtype=F32), vmem(2 * RC, QW, dtype=F32),
-] + [pltpu.SemaphoreType.DMA(s) for s in ((3,), (3,), (3, 3), (1,), (2, 8), (2, 4), (2,), (2,), (2, 4), (2,), (2, 4), (2, 4), (2, 4, 7), (2, 3), (2, 4), (2, 8))]
+] + [pltpu.SemaphoreType.DMA(s) for s in ((1,), (3,), (3, 3), (1,), (2, 8), (2, 4), (2,), (2,), (2, 4), (2,), (2, 4), (2, 4), (2, 4, 7), (2, 3), (2, 4), (2, 8))]
 
 
 def solution(mesh):
@@ -568,7 +566,6 @@
     anywhere = pl.BlockSpec(memory_space=pl.ANY)
 
     def local_forward(x, pos, w_q, w_k, w_v, w_o, w_gate, w_up, w_down, gain):
-        cosT, sinT = rope_tables(pos, HD)
         wq = w_q.transpose(0, 2, 3, 1).reshape(2, QW, DM)
         wk = w_k.transpose(0, 2, 3, 1).reshape(2, TOK, DM)
         wv = w_v.transpose(0, 2, 3, 1).reshape(2, TOK, DM)
@@ -576,12 +573,12 @@
         x, kT, vT = pl.pallas_call(
             stack_kernel,
             out_shape=tuple(pltpu.VMEM(s, BF16) for s in OUT_SHAPES),
-            in_specs=[anywhere, in_vmem] + [anywhere] * 9,
+            in_specs=[anywhere] + [in_vmem] * 2 + [anywhere] * 7,
             out_specs=(in_vmem,) * 3,
             scratch_shapes=SCRATCH,
             compiler_params=pltpu.CompilerParams(collective_id=0, has_side_effects=True, vmem_limit_bytes=VMEM_LIMIT),
             name='stack',
-        )(x, gain, cosT, sinT, wq, wk, wv, w_gate, w_up, w_down, wo)
+        )(x, gain, pos.reshape(1, TOK), wq, wk, wv, w_gate, w_up, w_down, wo)
         x, kT, vT = pl.pallas_call(
             finish_kernel,
             out_shape=tuple(jax.ShapeDtypeStruct(s, BF16) for s in OUT_SHAPES),

time: 144 us -> 140 us (0.972)
  Pallas kernels: 142 us -> 139 us
  other arithmetic: 1.52 us -> 0 us
    pallas_call x1, Pallas kernels: 141 us -> 138 us  [local_forward(): pl.pallas_call(stack_kernel, out_shape=tuple((pltpu.VMEM(s, BF16) for s i...]
where the time goes in v5:
time: 140 us
  Pallas kernels  139 us (99%)
    pallas_call x1, Pallas kernels, local_forward(): pl.pallas_call(stack_kernel, out_shape=tuple((pltpu.VMEM(s, BF16) for s i...  138 us

profile of v5, /device:TPU:121, one launch (start us, length us, event | category | flops | bytes accessed | tf_op | source)
XLA Modules:
  0.0 140.0 jit_solution(16684826647107704936)
XLA Ops:
  0.6 138.2 %stack.1 = (bf16[256,2048]{1,0:T(8,128)(2,1)S(1)}, bf16[2,256,256]{2,1,0:T(8,128)(2,1)S(1)}, bf16[2,256,256]{2,1,0:T(8,128)(2,1)S(1)}) custom-call(bf16[256,2048]{1,0:T(8,128)(2,1)} %x_hbm.1, bf16[2,2048]{1,0:T(2,128)(2,1)} %gain_ref.1, s32[1,256]{1,0:T(1,128)} %bitcast.21, bf16[2,1024,2048]{2,1,0:T(8,128)(2,1)} %bitcast.17, bf16[2,256,2048]{2,1,0:T(8,128)(2,1)} %bitcast.19, ...), custom_call_target="tpu_custom_call" | custom-call | tf_op jit(solution)/shard_map/stack/pallas_call | solution.py:573
  138.9 1.2 finish.1

commit v6 on v5

--- a/solution.py
+++ b/solution.py
@@ -27,7 +27,7 @@
 SENDS = ((0, ()), (1, ()), (1, (0,)), (2, ()), (2, (0,)), (2, (1,)), (2, (0, 1)))
 SECOND, THIRD = (1, 2), (3, 4, 5, 6)
 NEXT = ((2, 4), (5,), (6,), (), (), (), ())
-FOUR = range(4)
+FOUR, TWO, EIGHT = range(4), range(2), range(8)
 
 
 class Place:
@@ -41,7 +41,8 @@
         self.kv_local = 2 * self.mem[1] + self.mem[0]
         self.member = 2 * self.mem[2] + self.mem[1]
         same_z = 1 - lax.rem(self.head + self.mem[2], 2)
-        self.flag = same_z * (1 - lax.rem(self.head + self.core, 2))
+        self.own = 1 - lax.rem(self.head + self.core, 2)
+        self.flag = same_z * self.own
 
     def at(self, mem):
         cs = [m * 3 + c * (1 - 2 * m) for m, c in zip(mem, self.cls)]
@@ -74,8 +75,14 @@
         high = d[2] * (1 - self.core) + d[0] * self.core
         return self.at(mem) + low * (1 - self.mem[1]) + high * self.mem[1]
 
+    def is_member(self, i):
+        return (1 - lax.rem(i // 2 + self.mem[2], 2)) * (1 - lax.rem(i % 2 + self.mem[1], 2))
+
     def s_self(self, i):
-        return self.flag * (1 - lax.rem(i // 2 + self.mem[2], 2)) * (1 - lax.rem(i % 2 + self.mem[1], 2))
+        return self.flag * self.is_member(i)
+
+    def o_self(self, h):
+        return self.own * self.is_member(h // 2) * (1 - lax.rem(h % 2 + self.mem[0], 2))
 
     def t_self(self, t):
         return self.flag * (1 - lax.rem(t // 2 + self.mem[1], 2)) * (1 - lax.rem(t % 2 + self.mem[0], 2))
@@ -91,7 +98,7 @@
 
 def attn_logits(first, c, kv_all, qa, qb, sbuf, off, mx_ref, moff):
     cols = pl.ds(c * TOK, TOK)
-    keys = kv_all[pl.ds(first, NB), 0:LN, :].reshape(HALF, LN)
+    keys = kv_all[pl.ds(first, NB), :LN, :].reshape(HALF, LN)
     sa = jnp.dot(keys, qa[:, cols], preferred_element_type=F32) * (LOG2E / 8.0)
     sb = jnp.dot(keys, qb[:, cols], preferred_element_type=F32) * (LOG2E / 8.0)
     sbuf[pl.ds(off, HALF), cols] = sa
@@ -116,7 +123,7 @@
 
 
 def values_of(kv_all, first, blocks):
-    return [kv_all[first + b, LN + HD * h:192 + HD * h, :] for h in range(2) for b in range(blocks)]
+    return [kv_all[first + b, LN + HD * h:192 + HD * h, :] for h in TWO for b in range(blocks)]
 
 
 def attn_tail(first, t, kv_all, sbuf, off, m_ref, l_ref, acc_ref):
@@ -125,7 +132,7 @@
         ti = lax.broadcasted_iota(jnp.int32, (LN, TOK), 1)
         ki = lax.broadcasted_iota(jnp.int32, (LN, TOK), 0)
         parts = []
-        for h in range(2):
+        for h in TWO:
             base = pl.multiple_of(off + h * HALF, LN)
             if t > 0:
                 parts.append(sbuf[pl.ds(base, t * LN), cols])
@@ -208,7 +215,7 @@
         @pl.when(pos % NB == t)
         def _():
             attn_tail(pos // NB * NB, t, kv, sbuf, (groups % 2) * TK, m_ref.at[i], l_ref.at[i], acc_ref.at[i])
-    oT = acc_ref[i] / jnp.sum(l_ref[i], axis=0, keepdims=True)
+    oT = acc_ref[i] * (1.0 / jnp.sum(l_ref[i], axis=0, keepdims=True))
     halves = []
     for g in range(0, 4, 2):
         two = jnp.concatenate([oT[:, g * TOK:(g + 1) * TOK], oT[:, (g + 1) * TOK:(g + 2) * TOK]], axis=0)
@@ -240,7 +247,7 @@
 
     for c in start_cps:
         c.start()
-    for n in range(2):
+    for n in TWO:
         proj_copies(0)[n].start()
 
     barrier = pltpu.get_barrier_semaphore()
@@ -249,8 +256,11 @@
         pl.semaphore_signal(barrier, inc=1, device_id={'seq': seq, 'head': head}, device_id_type=MESH)
 
     for_others(me.s_self, lambda i: hello(me.source(i), me.mem[2]))
-    for_others(me.t_self, lambda t: hello(me.target(t), me.core))
-    for i in range(2):
+    for h in EIGHT:
+        @pl.when(me.o_self(h) == 0)
+        def _():
+            hello(me.at((h % 2, h // 2 % 2, h // 4)), me.core)
+    for i in TWO:
         hello(me.across(i, (0,)), me.mem[2])
     for step in me.steps(0, me.mem):
         hello(me.seq + step, me.head)
@@ -268,7 +278,7 @@
         for n in range(3):
             for c in gu_copies(layer, n):
                 c.start()
-        for n in range(2):
+        for n in TWO:
             d_copy(layer, n).start()
 
     freq = ROPE_BASE ** (-(lax.broadcasted_iota(jnp.int32, (HD // 2, TOK), 0).astype(F32) * 2.0 / HD))
@@ -280,7 +290,7 @@
     proj_copies(0)[2].start()
 
     def rope(a):
-        lo, hi = a[0:32], a[32:HD]
+        lo, hi = a[:32], a[32:HD]
         return jnp.concatenate([lo * cosT[:] - hi * sinT[:], hi * cosT[:] + lo * sinT[:]], axis=0)
 
     def project(w):
@@ -302,7 +312,7 @@
             k = rope(kT[t * HD:(t + 1) * HD].astype(F32)).astype(BF16)
             k_ref[layer, t * HD:(t + 1) * HD, :] = k
             kf = k.astype(F32)
-            kv_send[layer, t, 0:LN, :] = jnp.concatenate([kf[:, :LN], kf[:, LN:TOK]], axis=0).T.astype(BF16)
+            kv_send[layer, t, :LN, :] = jnp.concatenate([kf[:, :LN], kf[:, LN:TOK]], axis=0).T.astype(BF16)
             v = vT[t * HD:(t + 1) * HD]
             v_ref[layer, t * HD:(t + 1) * HD, :] = v
             kv_send[layer, t, LN:LN + HD, :] = v[:, :LN]
@@ -314,7 +324,7 @@
 
         @pl.when(layer == 0)
         def _():
-            pl.semaphore_wait(barrier, 12 - 2 * me.flag + 4 * (1 - me.mem[2]))
+            pl.semaphore_wait(barrier, 16 - me.flag - me.own + 4 * (1 - me.mem[2]))
 
         def kv_copy(t):
             return remote(kv_send.at[layer, t], kv.at[me.seq], skv.at[layer, t], rkv.at[layer, me.member], me.target(t), me.core)
@@ -397,7 +407,7 @@
 
         def add_down(hidden, n):
             d = jnp.dot(hidden, wdb[n % 3], preferred_element_type=F32)
-            for c in range(8):
+            for c in EIGHT:
                 part = d[:, c * TOK:(c + 1) * TOK]
                 mlp[layer, c] = part if n == 0 else mlp[layer, c] + part
 
@@ -422,27 +432,46 @@
             if n + 2 < N_TILES:
                 d_copy(layer, n + 2).start()
 
-        for n in range(1, BEFORE):
+        for n in range(1, N_TILES):
             for part, number in EVENTS.get(n, ()):
                 step(part, number)
             if n == 4:
                 send_queries()
             tile(n)
-
-        o_cp = pltpu.make_async_copy(wo.at[layer], wob, osem.at[0])
+        d_copy(layer, N_TILES - 1).wait()
+        add_down(hid[:], N_TILES - 1)
+
+        p_copy = remote(mlp.at[layer], part_in.at[layer], sp.at[layer], rp.at[layer], me.seq, sib)
+        p_copy.start()
+        half = pl.ds(pl.multiple_of(me.head * QW, QW), QW)
+        o_cp = pltpu.make_async_copy(wo.at[layer], wob.at[half], osem.at[0])
         o_cp.start()
+        wo_copy = remote(wob.at[half], wob.at[half], osem.at[1], osem.at[2], me.seq, sib)
 
         @pl.when(layer == 0)
         def _():
             for c in proj_copies(1):
                 c.start()
-        for part, number in EVENTS[BEFORE]:
-            step(part, number)
+            first_tiles(1)
         for_others(me.s_self, lambda i: remote(q_send.at[layer, 0], q_all.at[layer, i], sq.at[layer, 0], rq.at[layer, i], me.seq, sib).wait_recv())
         from_sibling(0)
 
-        def o_copy(i):
-            return remote(o_send.at[layer, i], o_full.at[layer, me.kv_local], so.at[layer, i], ro.at[layer, me.kv_local], me.source(i), me.mem[2])
+        def o_copy(i, head):
+            h = 4 * me.mem[2] + me.kv_local
+            return remote(o_send.at[layer, i], o_full.at[layer, h], so.at[layer, i, head], ro.at[layer, h], me.source(i), head)
+
+        def for_outputs(i, fn, at_home):
+            own = me.own * me.is_member(i)
+            for head in TWO:
+                here = own * (1 - lax.rem(me.head + head, 2))
+
+                @pl.when(here == 0)
+                def _():
+                    fn(i, head)
+
+                @pl.when(here == 1)
+                def _():
+                    at_home(i)
 
         lax.fori_loop(0, 4, lambda i, carry: attn_start(i, q_all[layer, i], state) or carry, 0)
         def early(n, carry):
@@ -450,8 +479,11 @@
             for e in FOUR:
                 @pl.when(n == e)
                 def _():
-                    for which, number in EVENTS[N_TILES + e]:
+                    for which, number in BREAKS[e]:
                         step(which, number)
+                    if e == 0:
+                        o_cp.wait()
+                        wo_copy.start()
                     if e == 1:
                         from_sibling(1)
             return carry
@@ -467,56 +499,50 @@
 
             @pl.when(i == 0)
             def _():
-                for part, number in EVENTS[N_TILES + 4]:
+                for part, number in BREAKS[4]:
                     step(part, number)
 
-            @pl.when(me.s_self(i) == 0)
+            def keep(i):
+                o_full[layer, 4 * me.mem[2] + me.kv_local] = o_send[layer, i]
+
+            for_outputs(i, lambda i, head: o_copy(i, head).start(), keep)
+            return carry
+
+        lax.fori_loop(0, 4, query, 0)
+
+        wo_copy.wait_send()
+        other = pl.ds(pl.multiple_of(sib * QW, QW), QW)
+        remote(wob.at[other], wob.at[other], osem.at[1], osem.at[2], me.seq, sib).wait_recv()
+        p_copy.wait_recv()
+        for h in EIGHT:
+            @pl.when(me.o_self(h) == 0)
             def _():
-                o_copy(i).start()
-
-            @pl.when(me.s_self(i) == 1)
-            def _():
-                o_full[layer, me.kv_local] = o_send[layer, i]
-            return carry
-
-        lax.fori_loop(0, 4, query, 0)
-        for n in range(BEFORE, N_TILES):
-            tile(n)
-        d_copy(layer, N_TILES - 1).wait()
-        add_down(hid[:], N_TILES - 1)
-
-        @pl.when(layer == 0)
-        def _():
-            first_tiles(1)
-
-        o_cp.wait()
-        for_others(me.t_self, lambda t: remote(o_send.at[layer, 0], o_full.at[layer, t], so.at[layer, 0], ro.at[layer, t], me.seq, sib).wait_recv())
-
-        def p_copy(n):
-            return remote(mlp.at[layer, n], part_in.at[layer, n], sp.at[layer], rp.at[layer, n], me.seq, sib)
-
-        heads = jnp.concatenate([o_full[layer, t] for t in FOUR], axis=1)
+                remote(o_send.at[layer, 0], o_full.at[layer, h], so.at[layer, 0, 0], ro.at[layer, h], me.seq, sib).wait_recv()
+
+        heads = jnp.concatenate([o_full[layer, h] for h in EIGHT], axis=1)
         for n in range(0, 8, 2):
             d = jnp.dot(heads, wob[:, n * TOK:(n + 2) * TOK], preferred_element_type=F32)
-            for e in range(2):
-                mlp[layer, n + e] += d[:, e * TOK:(e + 1) * TOK]
-                p_copy(n + e).start()
-        for n in range(8):
-            cols = pl.ds(n * TOK, TOK)
-            p_copy(n).wait_recv()
-            y = (mlp[layer, n] + part_in[layer, n]).astype(BF16)
-            x_ref[:, cols] = (x_ref[:, cols].astype(F32) + y.astype(F32)).astype(BF16)
+            for e in TWO:
+                cols = pl.ds((n + e) * TOK, TOK)
+                y = (mlp[layer, n + e] + part_in[layer, n + e] + d[:, e * TOK:(e + 1) * TOK]).astype(BF16)
+                x_ref[:, cols] = (x_ref[:, cols].astype(F32) + y.astype(F32)).astype(BF16)
         return carry
 
     lax.fori_loop(0, 2, layer_body, 0)
 
     def drain(layer, carry):
         def gone(src, sem):
-            remote(src, src, sem, rp.at[layer, 0], me.seq, sib).wait_send()
+            remote(src, src, sem, rp.at[layer], me.seq, sib).wait_send()
 
         for_others(me.t_self, lambda t: gone(kv_send.at[layer, t], skv.at[layer, t]))
         for_others(me.t_self, lambda t: gone(q_send.at[layer, t], sq.at[layer, t]))
-        for_others(me.s_self, lambda i: gone(o_send.at[layer, i], so.at[layer, i]))
+        for i in FOUR:
+            for head in TWO:
+                here = me.own * me.is_member(i) * (1 - lax.rem(me.head + head, 2))
+
+                @pl.when(here == 0)
+                def _():
+                    gone(o_send.at[layer, i], so.at[layer, i, head])
         gone(kv_all.at[layer, pl.ds(0, 26)], sag.at[layer])
 
         @pl.when(me.mem[2] == 0)
@@ -542,16 +568,16 @@
     return pltpu.VMEM(shape, dtype)
 
 
-BEFORE = 15
-EVENTS = {5: ((0, 0),), 7: ((1, 0),), 9: ((0, 2),), 11: ((1, 2),), 12: ((2, 0),), 13: ((0, 4),), 15: (), 16: ((1, 4), (2, 1)), 17: (), 18: ((2, 2),), 19: (), 20: ((2, 4),)}
+EVENTS = {5: ((0, 0),), 9: ((0, 2), (1, 0)), 12: ((1, 2), (2, 0)), 13: ((0, 4),)}
+BREAKS = (((1, 4), (2, 1)), (), ((2, 2),), (), ((2, 4),))
 
 
 SCRATCH = [
     vmem(32, TOK, dtype=F32), vmem(32, TOK, dtype=F32), vmem(TOK, DM), vmem(2, 4, TOK, TOK), vmem(2, 4, TOK, LN), vmem(2, 4, TOK, TOK), vmem(2, HD, TOK, LN),
-    vmem(2, 4, TOK, TOK), vmem(2, 4, TOK, TOK), vmem(2, 8, TOK, TOK, dtype=F32), vmem(2, 8, TOK, TOK, dtype=F32), vmem(TOK, TOK),
-    vmem(QW, DM), vmem(2 * TOK, DM), vmem(3, DM, TOK), vmem(3, DM, TOK), vmem(3, TOK, DM), vmem(QW, DM),
+    vmem(2, 4, TOK, TOK), vmem(2, 8, TOK, TOK), vmem(2, 8, TOK, TOK, dtype=F32), vmem(2, 8, TOK, TOK, dtype=F32), vmem(TOK, TOK),
+    vmem(QW, DM), vmem(2 * TOK, DM), vmem(3, DM, TOK), vmem(3, DM, TOK), vmem(3, TOK, DM), vmem(DM, DM),
     vmem(4, LN, QW), vmem(4, LN, QW), vmem(4, 8, QW, dtype=F32), vmem(4, RC, QW, dtype=F32), vmem(4, HD, QW, dtype=F32), vmem(2 * TK, QW, dtype=F32), vmem(2 * RC, QW, dtype=F32),
-] + [pltpu.SemaphoreType.DMA(s) for s in ((1,), (3,), (3, 3), (1,), (2, 8), (2, 4), (2,), (2,), (2, 4), (2,), (2, 4), (2, 4), (2, 4, 7), (2, 3), (2, 4), (2, 8))]
+] + [pltpu.SemaphoreType.DMA(s) for s in ((1,), (3,), (3, 3), (3,), (2, 8), (2, 4), (2,), (2,), (2, 4, 2), (2,), (2, 4), (2, 4), (2, 4, 7), (2, 3), (2, 8), (2,))]
 
 
 def solution(mesh):

time: 140 us -> 156 us (1.11); the launches traced: 140 us -> 154 us
  Pallas kernels: 139 us -> 154 us
    pallas_call x1, Pallas kernels: 138 us -> 153 us  [local_forward(): pl.pallas_call(stack_kernel, out_shape=tuple((pltpu.VMEM(s, BF16) for s i...]
where the time goes in v6:
time: 156 us; the launch traced here: 154 us
  Pallas kernels  154 us (99%)
    pallas_call x1, Pallas kernels, local_forward(): pl.pallas_call(stack_kernel, out_shape=tuple((pltpu.VMEM(s, BF16) for s i...  153 us

profile of v6, /device:TPU:121, one launch (start us, length us, event | category | flops | bytes accessed | tf_op | source)
XLA Modules:
  0.0 154.4 jit_solution(11458264975646817188)
XLA Ops:
  0.6 152.6 %stack.1 = (bf16[256,2048]{1,0:T(8,128)(2,1)S(1)}, bf16[2,256,256]{2,1,0:T(8,128)(2,1)S(1)}, bf16[2,256,256]{2,1,0:T(8,128)(2,1)S(1)}) custom-call(bf16[256,2048]{1,0:T(8,128)(2,1)} %x_hbm.1, bf16[2,2048]{1,0:T(2,128)(2,1)} %gain_ref.1, s32[1,256]{1,0:T(1,128)} %bitcast.21, bf16[2,1024,2048]{2,1,0:T(8,128)(2,1)} %bitcast.17, bf16[2,256,2048]{2,1,0:T(8,128)(2,1)} %bitcast.19, ...), custom_call_target="tpu_custom_call" | custom-call | tf_op jit(solution)/shard_map/stack/pallas_call | solution.py:599
  153.2 1.2 finish.1

commit v7 on v5

--- a/solution.py
+++ b/solution.py
@@ -9,7 +9,7 @@
 ROPE_BASE = 500000.0
 EPS = 1e-5
 LOG2E = 1.4426950408889634
-NEG = -1e30
+NEG = -3e38
 MESH = pl.DeviceIdType.MESH
 TOK, DM, QW, LN, HD = 256, 2048, 1024, 128, 64
 F32 = jnp.float32

time: 140 us -> 140 us (level)
  no operation moved by 1% of the time
where the time goes in v7:
time: 140 us
  Pallas kernels  139 us (99%)
    pallas_call x1, Pallas kernels, local_forward(): pl.pallas_call(stack_kernel, out_shape=tuple((pltpu.VMEM(s, BF16) for s i...  138 us

profile of v7, /device:TPU:121, one launch (start us, length us, event | category | flops | bytes accessed | tf_op | source)
XLA Modules:
  0.0 140.0 jit_solution(11360761313961331251)
XLA Ops:
  0.6 138.2 %stack.1 = (bf16[256,2048]{1,0:T(8,128)(2,1)S(1)}, bf16[2,256,256]{2,1,0:T(8,128)(2,1)S(1)}, bf16[2,256,256]{2,1,0:T(8,128)(2,1)S(1)}) custom-call(bf16[256,2048]{1,0:T(8,128)(2,1)} %x_hbm.1, bf16[2,2048]{1,0:T(2,128)(2,1)} %gain_ref.1, s32[1,256]{1,0:T(1,128)} %bitcast.21, bf16[2,1024,2048]{2,1,0:T(8,128)(2,1)} %bitcast.17, bf16[2,256,2048]{2,1,0:T(8,128)(2,1)} %bitcast.19, ...), custom_call_target="tpu_custom_call" | custom-call | tf_op jit(solution)/shard_map/stack/pallas_call | solution.py:573
  138.9 1.2 finish.1
